TPU v7x, 256 devices: a whole 4x4x8 slice. The times are simulated.
256 devices in a mesh: expert: 8 (over z), tp: 32 (over x, y, core).
Axes of the slice: x: 4, y: 4, z: 8, core: 2. Of those that a mesh axis runs over, the one named last changes fastest.
Arguments:
- tokens: bfloat16 [1024, 4096], P('expert', 'tp'), may hold values from -6 to 6
- norm_gain: bfloat16 [4096], replicated, may hold values from 0.5 to 1.5
- route_logits: float32 [1024, 2], P('expert'), may hold values from -6 to 6
- expert_ids: int32 [1024, 2], P('expert'), may hold values from 0 to 7, all different within a row; in each aligned block of 128 rows (0 to 127, 128 to 255, ...) at most 64 rows name the same one
- active: int32 [1024], P('expert'), may hold values 0 or 1
- gate_weight: bfloat16 [8, 14336, 4096], P('expert', 'tp'), may hold values from -0.09375 to 0.09375
- up_weight: bfloat16 [8, 14336, 4096], P('expert', 'tp'), may hold values from -0.09375 to 0.09375
- down_weight: bfloat16 [8, 14336, 4096], P('expert', 'tp'), may hold values from -0.046875 to 0.046875
Outputs:
- mixed: bfloat16 [1024, 4096], P('expert', 'tp')
Inputs may be any that keep to these rules, and one draw needn't show every extreme that they name: `expert_ids`: each token names 2 different experts. In each block of 128 consecutive token slots (the slots of one index of expert) no expert is named by more than 64 tokens, a bound that some block reaches. `active`: each entry is 0 or 1.
All inputs are finite; a program needn't handle non-finite values.
Results may differ from a plain program's by a relative error of at most 0.0025.
Values may be sent and summed in bfloat16 or wider, within the bound.
A program may use at most 64 MiB of HBM per device.

v0:
```python
import jax
import jax.numpy as jnp
from jax import lax
from jax.sharding import Mesh
from jax.sharding import PartitionSpec as P

TP = ("tp_0", "tp_1", "tp_2")


epsilon = 1e-05


def one_axis_at_a_time(shard, axes):
    for axis in axes:
        shard = lax.psum(shard, axis)
    return shard


def taken_in(shard, axis, dim, absorb, state):
    everything = jax.tree.map(lambda a: lax.all_gather(a, axis, axis=dim, tiled=True), shard)
    return absorb(state, everything, jnp.int32(0))


def own_rows(product, width, axis):
    everything = product(jnp.int32(0), lax.axis_size(axis) * width)
    own = lax.psum_scatter(everything, axis, scatter_dimension=0, tiled=True)
    return own


def slot_numbers(expert_ids, active, seat_limit, experts):
    flat_ids = expert_ids.reshape(-1)
    is_live = jnp.broadcast_to(active[:, None], expert_ids.shape).reshape(-1)
    columns = jnp.arange(experts, dtype=jnp.int32)
    one_hot = (flat_ids[:, None] == columns[None, :]).astype(jnp.int32) * is_live[:, None]
    earlier = jnp.cumsum(one_hot, axis=0) - one_hot
    position = jnp.sum(earlier * one_hot, axis=1)
    slot_index = jnp.where(is_live > 0, flat_ids * seat_limit + position, -1)
    return slot_index.reshape(expert_ids.shape)


def local(tokens, norm_gain, route_logits, expert_ids, active, gate_weight, up_weight, down_weight):
    expert_count = lax.axis_size("expert")
    tp_index = lax.axis_index(TP)
    token_count, feature_share = tokens.shape
    local_count, ff_share, model_width = gate_weight.shape
    seat_limit = token_count // 2
    experts = expert_count * local_count
    slots = expert_count * seat_limit
    gains = norm_gain.astype(jnp.float32)
    widened = tokens.astype(jnp.float32)
    squares = one_axis_at_a_time(jnp.sum(widened * widened, axis=1), TP)
    gain_part = lax.dynamic_slice_in_dim(gains, tp_index * feature_share, feature_share)
    mean_square = squares[:, None] / model_width
    normed = (widened * lax.rsqrt(mean_square + epsilon) * gain_part).astype(jnp.bfloat16)
    route_probs = jax.nn.softmax(route_logits, axis=1) * active.astype(jnp.float32)[:, None]
    slot_index = slot_numbers(expert_ids, active, seat_limit, experts)
    buffer_rows = experts * seat_limit
    targets = jnp.arange(buffer_rows, dtype=jnp.int32)
    pick_hot = (slot_index[:, :, None] == targets[None, None, :]).astype(jnp.bfloat16)
    send_hot = jnp.sum(pick_hot, axis=1)
    send_rows = jnp.einsum(
        "jr,jw->rw", send_hot, normed, preferred_element_type=jnp.float32
    ).astype(jnp.bfloat16)
    arriving = lax.all_to_all(send_rows, "expert", split_axis=0, concat_axis=0, tiled=True)
    received = arriving.reshape(expert_count, local_count, seat_limit, -1).transpose(1, 0, 2, 3)
    received = received.reshape(local_count, slots, -1)
    empty = jnp.zeros((local_count, slots, ff_share), jnp.float32)

    def add_projections(running, shard_piece, offset):
        sequence_extent = shard_piece.shape[2]
        gate_part = lax.dynamic_slice_in_dim(gate_weight, offset, sequence_extent, 2)
        up_part = lax.dynamic_slice_in_dim(up_weight, offset, sequence_extent, 2)
        gate_next = running[0] + jnp.einsum(
            "lrd,lfd->lrf", shard_piece, gate_part, preferred_element_type=jnp.float32
        )
        up_next = running[1] + jnp.einsum(
            "lrd,lfd->lrf", shard_piece, up_part, preferred_element_type=jnp.float32
        )
        return (gate_next, up_next)

    gate_sum, up_sum = taken_in(received, TP, 2, add_projections, (empty, empty))
    inner_width = (jax.nn.silu(gate_sum) * up_sum).astype(jnp.bfloat16)

    def down_terms(offset, count):
        lowering_share = lax.dynamic_slice_in_dim(down_weight, offset, count, 2)
        return jnp.einsum(
            "hzj,hjs->shz", inner_width, lowering_share, preferred_element_type=jnp.float32
        )

    reduced = own_rows(down_terms, feature_share, TP)
    specialist_result = reduced.transpose(1, 2, 0).astype(jnp.bfloat16)
    returning = specialist_result.reshape(
        local_count, expert_count, seat_limit, feature_share
    ).transpose(1, 0, 2, 3)
    returning = returning.reshape(expert_count * local_count * seat_limit, feature_share)
    arrived = lax.all_to_all(returning, "expert", split_axis=0, concat_axis=0, tiled=True)
    picked = jnp.einsum("jkr,rw->jkw", pick_hot, arrived, preferred_element_type=jnp.float32)
    mixed = jnp.sum(route_probs[:, :, None] * picked, axis=1)
    return mixed.astype(jnp.bfloat16)


def solution(mesh):
    split = Mesh(
        mesh.devices.reshape(mesh.shape["expert"], 4, 4, 2), ("expert", "tp_0", "tp_1", "tp_2")
    )
    in_specs = (
        P("expert", TP),
        P(),
        P("expert", None),
        P("expert", None),
        P("expert"),
        P("expert", TP, None),
        P("expert", TP, None),
        P("expert", TP, None),
    )
    out_specs = P("expert", TP)
    return jax.shard_map(local, mesh=split, in_specs=in_specs, out_specs=out_specs, check_vma=False)
```

profile of v0, /device:TPU:2, one launch (start us, length us, event | category | flops | bytes accessed | tf_op | source)
XLA Modules:
  0.0 243.9 jit_solution(12486279213063765660)
XLA Ops:
  6.5 0.0 all-gather.2.cloned.1.call-start
  6.5 0.8 copy.19
  7.3 0.1 eq.38
  7.5 0.1 eq.42
  7.6 0.7 broadcast_in_dim.27
  8.3 0.7 broadcast_compare_fusion
  9.0 0.1 broadcast_in_dim.28
  9.1 0.1 broadcast_in_dim.29
  9.2 0.6 reduce-window.6
  9.8 0.2 slice_reduce_fusion
  10.1 0.7 broadcast_in_dim.30
  10.8 0.1 mul.85
  11.0 0.1 fusion.36
  11.1 0.1 reduce_sum.52
  11.2 0.1 copy.21
  11.3 0.7 add_select_fusion
  12.0 0.1 fusion.28
  12.1 0.9 fusion.30
  13.0 9.9 %psum.21 = f32[128]{0:T(128)S(1)} all-reduce(f32[128]{0:T(128)S(1)} %fusion.30), channel_id=1, replica_groups=mesh['expert'=8,'tp_0'=4,'tp_1'=4,'tp_2'=2] {'tp_0'}, use_global_device_ids=true, to_apply=%region_7.8 | all-reduce | flops 128 | bytes 1024 | tf_op jit(solution)/shard_map/psum | solution.py:15
  22.9 9.4 %psum.22 = f32[128]{0:T(128)S(1)} all-reduce(f32[128]{0:T(128)S(1)} %psum.21), channel_id=1, replica_groups=mesh['expert'=8,'tp_0'=4,'tp_1'=4,'tp_2'=2] {'tp_1'}, use_global_device_ids=true, to_apply=%region_8.9 | all-reduce | flops 128 | bytes 1024 | tf_op jit(solution)/shard_map/psum | solution.py:15
  32.3 2.5 %psum.23 = f32[128]{0:T(128)S(1)} all-reduce(f32[128]{0:T(128)S(1)} %psum.22), channel_id=1, replica_groups=mesh['expert'=8,'tp_0'=4,'tp_1'=4,'tp_2'=2] {'tp_2'}, use_global_device_ids=true, to_apply=%region_9.10 | all-reduce | flops 128 | bytes 1024 | tf_op jit(solution)/shard_map/psum | solution.py:15
  34.8 0.8 dynamic-slice_convert_fusion
  35.5 1.0 convolution_convert_fusion
  36.5 17.6 %all_to_all.21 = bf16[8,64,128]{2,1,0:T(8,128)(2,1)} all-to-all(bf16[8,64,128]{2,1,0:T(8,128)(2,1)S(1)} %bitcast.45), channel_id=1, replica_groups=mesh['expert'=8,'tp_0'=4,'tp_1'=4,'tp_2'=2] {'expert'}, dimensions={0} | all-to-all | bytes 262144 | tf_op jit(solution)/shard_map/all_to_all | solution.py:64
  54.1 0.0 all-gather.2.cloned.1.call-update
  54.2 0.0 reduce-scatter.2.cloned.1.call-start
  54.2 46.9 %all-gather.2.cloned.1.call-done = bf16[1,512,4096]{2,1,0:T(8,128)(2,1)} async-done(((bf16[1,512,128]{2,1,0:T(8,128)(2,1)}), bf16[1,512,4096]{2,1,0:T(8,128)(2,1)}) %all-gather.2.cloned.1.call-update) | async-done | bytes 4194320 | tf_op jit(solution)/shard_map/all_gather | solution.py:20
  101.1 5.4 %fusion.2 = f32[512,448]{0,1:T(8,128)S(1)} fusion(bf16[1,512,4096]{2,1,0:T(8,128)(2,1)} %all-gather.2.cloned.1.call-done, bf16[1,448,4096]{2,1,0:T(8,128)(2,1)} %param.13), kind=kOutput, calls=%fused_computation.3 | convolution fusion | flops 1879048192 | bytes 8781824 | tf_op jit(solution)/shard_map/lrd,lfd->lrf/dot_general | solution.py:73
  106.6 12.0 %convolution_bitcast_fusion = f32[4096,1,512]{0,2,1:T(8,128)} fusion(bf16[1,448,4096]{2,1,0:T(8,128)(2,1)} %param.15, bf16[1,448,4096]{2,1,0:T(8,128)(2,1)} %param.14, bf16[1,512,4096]{2,1,0:T(8,128)(2,1)} %all-gather.2.cloned.1.call-done, f32[512,448]{0,1:T(8,128)S(1)} %fusion.2), kind=kOutput, calls=%fused_computation | convolution fusion | flops 3759472640 | bytes 20840448 | tf_op jit(solution)/shard_map/hzj,hjs->shz/dot_general | solution.py:86
  118.6 0.0 copy-start
  118.6 0.0 copy-start.1
  118.6 0.0 reduce-scatter.2.cloned.1.call-update
  118.6 0.7 copy-done
  119.3 99.5 %reduce-scatter.2.cloned.1.call-done = f32[128,1,512]{0,2,1:T(8,128)} async-done(((f32[4096,1,512]{0,2,1:T(8,128)}), f32[128,1,512]{0,2,1:T(8,128)}) %reduce-scatter.2.cloned.1.call-update) | async-done | bytes 262160 | tf_op jit(solution)/shard_map/reduce_scatter | solution.py:26
  218.7 1.6 convert_element_type.41
  220.3 7.1 %all-to-all-start.1 = ((bf16[8,64,128]{2,1,0:T(8,128)(2,1)}), bf16[8,64,128]{2,1,0:T(8,128)(2,1)S(1)}, u32[]{:S(2)}, u32[]{:S(2)}) async-start(bf16[8,64,128]{2,1,0:T(8,128)(2,1)} %bitcast.11), calls=%async_computation.2 | async-start | bytes 262144 | tf_op jit(solution)/shard_map/all_to_all | solution.py:96
  227.4 0.0 copy-done.1
  227.5 8.7 %all-to-all-done.1 = bf16[8,64,128]{2,1,0:T(8,128)(2,1)S(1)} async-done(((bf16[8,64,128]{2,1,0:T(8,128)(2,1)}), bf16[8,64,128]{2,1,0:T(8,128)(2,1)S(1)}, u32[]{:S(2)}, u32[]{:S(2)}) %all-to-all-start.1) | async-done | bytes 131104 | tf_op jit(solution)/shard_map/all_to_all | solution.py:96
  236.2 0.9 fusion.17
  (8 shorter events, 0.1 us)
Async XLA Ops:
  6.5 94.6 %all-gather.2.cloned.1.call-start = ((), (), s32[]{:S(2)}) async-start(), calls=%async_computation.3 | async-start | bytes 4325376 | tf_op jit(solution)/shard_map/all_gather | solution.py:20
  54.2 164.6 %reduce-scatter.2.cloned.1.call-start = ((), (), s32[]{:S(2)}) async-start(), calls=%async_computation.4 | async-start | bytes 8650752 | tf_op jit(solution)/shard_map/reduce_scatter | solution.py:26
  118.6 0.7 copy-start
  118.6 108.9 %copy-start.1 = (s32[128]{0:T(128)S(1)}, s32[128]{0:T(128)}, u32[]{:S(2)}) copy-start(s32[128]{0:T(128)} %param.12) | copy-start | bytes 1540
  220.3 15.8 %all-to-all-start.1 = ((bf16[8,64,128]{2,1,0:T(8,128)(2,1)}), bf16[8,64,128]{2,1,0:T(8,128)(2,1)S(1)}, u32[]{:S(2)}, u32[]{:S(2)}) async-start(bf16[8,64,128]{2,1,0:T(8,128)(2,1)} %bitcast.11), calls=%async_computation.2 | async-start | bytes 262144 | tf_op jit(solution)/shard_map/all_to_all | solution.py:96
Sparse Core Ops, SparseCore 0:
  54.3 46.8 all-gather.1
  118.7 99.9 reduce-scatter.1
where the time goes:
time: 244 us
  waiting for transfers between devices  155 us (64%)
  blocking collectives  39.4 us (16%)
  matrix products  19.3 us (8%)
  between operations  13.5 us (6%)
  starting transfers between devices  7.11 us (3%)
  other arithmetic  5.48 us (2%)
  local copies, waits for them, and re-layouts  3.98 us (2%)
    reduce_scatter x1, waiting for transfers between devices, own_rows(): own = lax.psum_scatter(everything, axis, scatter_dimension=0, tiled=True)  99.5 us
    all_gather x1, waiting for transfers between devices, taken_in(): lax.all_gather(a, axis, axis=dim, tiled=True)  46.9 us
    psum x3, blocking collectives, one_axis_at_a_time(): shard = lax.psum(shard, axis)  21.8 us
    all_to_all x1, blocking collectives, local(): lax.all_to_all(send_rows, 'expert', split_axis=0, concat_axis=0, tiled=True)  17.6 us
    dot_general x1, matrix products, down_terms(): jnp.einsum('hzj,hjs->shz', inner_width, lowering_share, preferred_element...  12 us
    all_to_all x1, waiting for transfers between devices, local(): lax.all_to_all(returning, 'expert', split_axis=0, concat_axis=0, tiled=True)  8.7 us
    all_to_all x1, starting transfers between devices, local(): lax.all_to_all(returning, 'expert', split_axis=0, concat_axis=0, tiled=True)  7.07 us
    dot_general x1, matrix products, add_projections(): jnp.einsum('lrd,lfd->lrf', shard_piece, gate_part, preferred_element_type...  5.41 us
  transfers between devices with their start and end apart: 3, of which 3 were waited for; matrix products, arithmetic and copies ran while one was open for 0% of the time, Pallas kernels for 0%

commit v1 on v0

v1 whole, which is shorter than its diff:
```python
import jax
import jax.numpy as jnp
from jax import lax
from jax.experimental import pallas as pl
from jax.experimental.pallas import tpu as pltpu
from jax.sharding import Mesh
from jax.sharding import PartitionSpec as P

MESH = pl.DeviceIdType.MESH
EPS = 1e-05
ZS = 8
SIDE = 4
SEATS = 64
ROWS = ZS * SEATS
HALF = ROWS // 2
FEAT = 128
HID = 448
WIDTH = 4096
QROWS = HALF + 16
QMAX = 32000.0

ORDER = [(0, 0), (3, 0), (1, 0), (0, 3), (0, 1), (2, 0), (3, 3), (3, 1), (1, 3), (1, 1), (0, 2), (2, 3), (2, 1), (3, 2), (1, 2), (2, 2)]
PRODUCTS = {6: ((0, 1), (3, 2)), 8: ((4, 6),), 9: ((7, 8),), 11: ((9, 5),), 14: ((10, 11), (13, 12)), 15: ((14, 15),)}


def encode(v, ref):
    top = jnp.maximum(jnp.max(jnp.abs(v), axis=0, keepdims=True), 1e-30)
    exponent = jnp.ceil(jnp.log2(top))
    power = jnp.exp2(exponent)
    mantissa = jnp.ceil(top / power * QMAX)
    inverse = (QMAX * QMAX) / (mantissa * power)
    ref[0:HALF, :] = jnp.round(v * inverse).astype(jnp.int32).astype(jnp.int16)
    row = lax.broadcasted_iota(jnp.int32, (16, FEAT), 0)
    scale = jnp.where(row < 8, exponent.astype(jnp.int32), mantissa.astype(jnp.int32))
    ref[HALF:QROWS, :] = scale.astype(jnp.int16)


def decode(ref):
    scale = ref[HALF:QROWS, :].astype(jnp.int32).astype(jnp.float32)
    factor = scale[8:9, :] * jnp.exp2(scale[0:1, :]) * (1.0 / (QMAX * QMAX))
    return ref[0:HALF, :].astype(jnp.int32).astype(jnp.float32) * factor


def column(row):
    return jnp.broadcast_to(row, (FEAT, FEAT)).T


def dot(a, b, dims, precision=None):
    return lax.dot_general(a, b, (dims, ((), ())), precision=precision, preferred_element_type=jnp.float32)


def kernel(
    tok_ref, gain_ref, logit_ref, ids_ref, act_ref, wg_hbm, wu_hbm, wd_hbm, out_ref,
    wg, wu, dn, outbox, gathered, scale_rows, rsend, rrecv, turned, msb, xn, gate, up, hid, part, red,
    sfb, sdb, rfb, rdb, sfa, sda, rfa, rda, fin, ret,
    w_sem, dn_sem, dns_sem, dnr_sem, z_s, z_r, rz_s, rz_r, ms_s, ms_r, g_s, g_r, d_s, d_r, h_s, h_r,
    b_s, bf_r, bd_r, a_s, af_r, ad_r, t_s, t_r,
):
    z, x, y, c = (lax.axis_index(n) for n in ("expert", "x", "y", "c"))
    a = jnp.where(c == 0, x, y)
    b = jnp.where(c == 0, y, x)
    mate = {"c": 1 - c}
    pending = []

    def wrap(v):
        return lax.rem(v, SIDE)

    def to_a(s):
        return {"x": wrap(x + s * (1 - c)), "y": wrap(y + s * c)}

    def to_b(s):
        return {"x": wrap(x + s * c), "y": wrap(y + s * (1 - c))}

    def to_z(s):
        return {"expert": lax.rem(z + s, ZS)}

    def remote(src, dst, s_sem, r_sem, device, start=True):
        copy = pltpu.make_async_remote_copy(src_ref=src, dst_ref=dst, send_sem=s_sem, recv_sem=r_sem, device_id=device, device_id_type=MESH)
        if start:
            copy.start()
            pending.append(copy)
        return copy

    def arrived(ref, sem):
        pltpu.make_async_copy(ref, ref, sem).wait()

    loads = [pltpu.make_async_copy(wg_hbm, wg, w_sem.at[0]), pltpu.make_async_copy(wu_hbm, wu, w_sem.at[1])]
    for copy in loads:
        copy.start()

    def down_columns(aa, bb, core):
        xx = jnp.where(core == 0, aa, bb)
        yy = jnp.where(core == 0, bb, aa)
        return pl.ds(pl.multiple_of(((xx * SIDE + yy) * 2 + core) * FEAT, FEAT), FEAT)

    barrier = pltpu.get_barrier_semaphore()
    peers = [mate] + [{"x": wrap(x + s)} for s in (1, 2, 3)] + [{"y": wrap(y + s)} for s in (1, 2, 3)] + [to_z(s) for s in range(1, ZS)]
    for peer in peers:
        pl.semaphore_signal(barrier, inc=1, device_id=peer, device_id_type=MESH)

    for aa in range(SIDE):
        for bb in range(SIDE):
            pltpu.make_async_copy(wd_hbm.at[:, down_columns(aa, bb, c)], dn.at[c, bb, :, pl.ds(aa * FEAT, FEAT)], dn_sem).start()

    tok = tok_ref[...]
    wide = tok.astype(jnp.float32)
    squares = jnp.sum((wide * wide).T, axis=0, keepdims=True)
    msb[0] = squares

    seat_row = lax.broadcasted_iota(jnp.int32, (ROWS, FEAT), 0)
    expert_of = seat_row // SEATS
    seat_of = (seat_row - expert_of * SEATS).astype(jnp.float32)
    live = jnp.broadcast_to(act_ref[...], (ROWS, FEAT)) > 0
    first = (expert_of == jnp.broadcast_to(ids_ref[0:1, :], (ROWS, FEAT))) & live
    second = (expert_of == jnp.broadcast_to(ids_ref[1:2, :], (ROWS, FEAT))) & live
    named = jnp.where(first | second, 1.0, 0.0)
    before = jnp.where(lax.broadcasted_iota(jnp.int32, (FEAT, FEAT), 0) < lax.broadcasted_iota(jnp.int32, (FEAT, FEAT), 1), 1.0, 0.0)
    position = dot(named.astype(jnp.bfloat16), before.astype(jnp.bfloat16), ((1,), (0,)))
    seated = position == seat_of
    pick0 = jnp.where(first & seated, 1.0, 0.0)
    pick1 = jnp.where(second & seated, 1.0, 0.0)
    pick = (pick0 + pick1).astype(jnp.bfloat16)
    outbox[...] = dot(pick, tok, ((1,), (0,))).astype(jnp.bfloat16)

    pl.semaphore_wait(barrier, len(peers))

    remote(msb.at[0], msb.at[1], ms_s.at[0], ms_r.at[0], mate)
    me = a * SIDE + b
    for s in range(1, ZS):
        target = lax.rem(z + s, ZS)
        remote(
            outbox.at[pl.ds(pl.multiple_of(target * SEATS, SEATS), SEATS)],
            gathered.at[c, me, pl.ds(pl.multiple_of(z * SEATS, SEATS), SEATS)],
            z_s.at[s - 1], z_r.at[s - 1], to_z(s),
        )
    own_seats = pl.ds(pl.multiple_of(z * SEATS, SEATS), SEATS)
    gathered[c, me, own_seats, :] = outbox[own_seats, :]
    for aa in range(SIDE):
        for bb in range(SIDE):
            remote(wd_hbm.at[:, down_columns(aa, bb, 1 - c)], dn.at[c, bb, :, pl.ds(aa * FEAT, FEAT)], dns_sem, dnr_sem, mate)
            pending.pop()
    arrived(msb.at[1], ms_r.at[0])
    msb[2] = msb[0] + msb[1]
    for s in (1, 2, 3):
        remote(msb.at[2], msb.at[2 + s], ms_s.at[s], ms_r.at[s], {"x": wrap(x + s)})

    count = [0]

    def pass_on(i, j, half, device):
        k = wrap(a + i) * SIDE + wrap(b + j)
        ref = gathered.at[c, k, pl.ds(half * HALF, HALF)]
        n = count[0]
        count[0] += 1
        remote(ref, ref, g_s.at[n], g_r.at[k * 2 + half], device)

    def await_half(i, j, half):
        k = wrap(a + i) * SIDE + wrap(b + j)
        arrived(gathered.at[c, k, pl.ds(half * HALF, HALF)], g_r.at[k * 2 + half])

    def arrive(n):
        i, j = ORDER[n]
        if (i, j) == (0, 0):
            for s in range(1, ZS):
                arrived(gathered.at[c, me, pl.ds(0, SEATS)], z_r.at[s - 1])
            for h in (0, 1):
                pass_on(0, 0, h, to_a(1))
                pass_on(0, 0, 1 - h, to_a(3))
        elif j == 0:
            if i == 3:
                await_half(i, 0, 0)
                pass_on(i, 0, 0, to_a(1))
                await_half(i, 0, 1)
            elif i == 1:
                await_half(i, 0, 1)
                pass_on(i, 0, 1, to_a(3))
                await_half(i, 0, 0)
            else:
                await_half(i, 0, 0)
                await_half(i, 0, 1)
        elif j == 3:
            await_half(i, j, 0)
            pass_on(i, j, 0, to_b(1))
            await_half(i, j, 1)
        elif j == 1:
            await_half(i, j, 1)
            pass_on(i, j, 1, to_b(3))
            await_half(i, j, 0)
        else:
            await_half(i, j, 0)
            await_half(i, j, 1)
        if j == 0:
            for h in (0, 1):
                pass_on(i, 0, h, to_b(1))
                pass_on(i, 0, 1 - h, to_b(3))
        k = wrap(a + i) * SIDE + wrap(b + j)
        remote(gathered.at[c, k], gathered.at[c, k], d_s.at[n], d_r.at[k], mate)

    def product(group, opening):
        offsets = []
        for p, n in enumerate(group):
            i, j = ORDER[n]
            aa, bb = wrap(a + i), wrap(b + j)
            mine, other = aa * SIDE + bb, bb * SIDE + aa
            arrived(gathered.at[1 - c, other], d_r.at[other])
            chip = jnp.where(c == 0, mine, other)
            gains = gain_ref[chip]
            for core in (0, 1):
                k = jnp.where(c == core, mine, other)
                raw = gathered[core, k].astype(jnp.float32)
                lanes = slice(core * FEAT, (core + 1) * FEAT)
                normed = raw * scale_rows[...] * gains[:, lanes].astype(jnp.float32)
                xn[p, :, lanes] = normed.astype(jnp.bfloat16)
            offsets.append(pl.ds(pl.multiple_of(chip * 2 * FEAT, 2 * FEAT), 2 * FEAT))
        for w, total in ((wg, gate), (wu, up)):
            terms = sum(dot(xn[p], w[:, at], ((1,), (1,))) for p, at in enumerate(offsets))
            total[...] = terms if opening else total[...] + terms

    arrived(msb.at[3], ms_r.at[1])
    arrived(msb.at[4], ms_r.at[2])
    arrived(msb.at[5], ms_r.at[3])
    msb[6] = (msb[2] + msb[3]) + (msb[4] + msb[5])
    for s in (1, 2, 3):
        remote(msb.at[6], msb.at[6 + s], ms_s.at[3 + s], ms_r.at[3 + s], {"y": wrap(y + s)})
    arrive(0)
    for s in (1, 2, 3):
        arrived(msb.at[6 + s], ms_r.at[3 + s])
    mean_square = ((msb[6] + msb[7]) + (msb[8] + msb[9])) / WIDTH
    inverse = lax.rsqrt(mean_square + EPS)
    rsend[...] = dot(jnp.broadcast_to(inverse, (8, FEAT)), pick.astype(jnp.float32), ((1,), (1,)), lax.Precision.HIGHEST)[0:1, :]
    for s in range(1, ZS):
        remote(rsend, rrecv.at[z], rz_s.at[s - 1], rz_r.at[s - 1], to_z(s))
    rrecv[z] = rsend[...]

    l0, l1 = logit_ref[0:1, :], logit_ref[1:2, :]
    high = jnp.maximum(l0, l1)
    e0, e1 = jnp.exp(l0 - high), jnp.exp(l1 - high)
    alive = act_ref[...].astype(jnp.float32)
    prob0 = column(e0 / (e0 + e1) * alive)
    prob1 = column(e1 / (e0 + e1) * alive)

    arrive(1)
    arrive(2)
    arrive(3)
    arrive(4)
    for s in range(1, ZS):
        arrived(rrecv.at[z], rz_r.at[s - 1])
    lane_block = pl.ds(pl.multiple_of(z // 2 * FEAT, FEAT), FEAT)
    seat_block = pl.ds(pl.multiple_of(z % 2 * SEATS, SEATS), SEATS)
    for g in range(ZS):
        turned[...] = column(rrecv[g, :, lane_block])
        scale_rows[g * SEATS : (g + 1) * SEATS, :] = turned[seat_block, :]
    for copy in loads:
        copy.wait()
    opening = True
    for n in range(5, 16):
        arrive(n)
        for group in PRODUCTS.get(n, ()):
            product(group, opening)
            opening = False

    quarter = ROWS // 4
    for q in range(4):
        rows = slice(q * quarter, (q + 1) * quarter)
        g = gate[rows, :]
        hid[c, rows, :] = (g / (1.0 + jnp.exp(-g)) * up[rows, :]).astype(jnp.bfloat16)
        ref = hid.at[c, pl.ds(q * quarter, quarter)]
        remote(ref, ref, h_s.at[q], h_r.at[q], mate)
    arrived(dn.at[c], dn_sem)
    arrived(dn.at[1 - c], dnr_sem)
    for q in range(4):
        arrived(hid.at[1 - c, pl.ds(q * quarter, quarter)], h_r.at[q])

    def partial(j):
        bb = wrap(b + j)
        part[j] = dot(hid[0], dn[0, bb], ((1,), (0,))) + dot(hid[1], dn[1, bb], ((1,), (0,)))

    LO, HI = slice(0, HALF), slice(HALF, ROWS)

    def lanes_of(i):
        return pl.ds(pl.multiple_of(wrap(a + i) * FEAT, FEAT), FEAT)

    ahead = (2, 3, 1, 0)
    partial(2)
    for i in ahead:
        aa = wrap(a + i)
        for d, rows, step in ((0, LO, 1), (1, HI, 3)):
            encode(part[2, rows, lanes_of(i)], sfb.at[d, aa])
            remote(sfb.at[d, aa], rfb.at[d, aa], b_s.at[0, d, aa], bf_r.at[d, aa], to_b(step))
    partial(1)
    partial(3)
    partial(0)
    for i in ahead:
        aa = wrap(a + i)
        for d, j, rows, h, step in ((0, 1, HI, 1, 1), (1, 3, LO, 0, 3)):
            encode(part[j, rows, lanes_of(i)], sdb.at[d, aa, h])
            remote(sdb.at[d, aa, h], rdb.at[d, aa, h], b_s.at[1, d, aa], bd_r.at[d, aa, h], to_b(step))
        for d, j, rows, h, step in ((0, 1, LO, 0, 1), (1, 3, HI, 1, 3)):
            arrived(rfb.at[d, aa], bf_r.at[d, aa])
            encode(part[j, rows, lanes_of(i)] + decode(rfb.at[d, aa]), sdb.at[d, aa, h])
            remote(sdb.at[d, aa, h], rdb.at[d, aa, h], b_s.at[2, d, aa], bd_r.at[d, aa, h], to_b(step))

    def finish_b(i, h):
        aa = wrap(a + i)
        rows = LO if h == 0 else HI
        arrived(rdb.at[0, aa, h], bd_r.at[0, aa, h])
        arrived(rdb.at[1, aa, h], bd_r.at[1, aa, h])
        return part[0, rows, lanes_of(i)] + decode(rdb.at[0, aa, h]) + decode(rdb.at[1, aa, h])

    for d, step in ((0, 1), (1, 3)):
        encode(finish_b(2, d), sfa.at[d])
        remote(sfa.at[d], rfa.at[d], a_s.at[0, d], af_r.at[d], to_a(step))
    for d, i, h, step in ((0, 1, 1, 1), (1, 3, 0, 3)):
        encode(finish_b(i, h), sda.at[d, h])
        remote(sda.at[d, h], rda.at[d, h], a_s.at[1, d], ad_r.at[d, h], to_a(step))
    for d, i, h, step in ((0, 1, 0, 1), (1, 3, 1, 3)):
        value = finish_b(i, h)
        arrived(rfa.at[d], af_r.at[d])
        encode(value + decode(rfa.at[d]), sda.at[d, h])
        remote(sda.at[d, h], rda.at[d, h], a_s.at[2, d], ad_r.at[d, h], to_a(step))
    red[0] = finish_b(0, 0)
    red[1] = finish_b(0, 1)
    for h in (0, 1):
        arrived(rda.at[0, h], ad_r.at[0, h])
        arrived(rda.at[1, h], ad_r.at[1, h])
        fin[h * HALF : (h + 1) * HALF, :] = (red[h] + decode(rda.at[0, h]) + decode(rda.at[1, h])).astype(jnp.bfloat16)

    for s in range(1, ZS):
        target = lax.rem(z + s, ZS)
        remote(
            fin.at[pl.ds(pl.multiple_of(target * SEATS, SEATS), SEATS)],
            ret.at[own_seats],
            t_s.at[s - 1], t_r.at[s - 1], to_z(s),
        )
    ret[own_seats, :] = fin[own_seats, :]
    for s in range(1, ZS):
        arrived(ret.at[pl.ds(0, SEATS)], t_r.at[s - 1])
    back = ret[...]
    from0 = dot(pick0.astype(jnp.bfloat16), back, ((0,), (0,)))
    from1 = dot(pick1.astype(jnp.bfloat16), back, ((0,), (0,)))
    out_ref[...] = (prob0 * from0 + prob1 * from1).astype(jnp.bfloat16)

    for copy in pending:
        copy.wait_send()
    arrived(dn.at[c], dns_sem)


def local(tokens, norm_gain, route_logits, expert_ids, active, gate_weight, up_weight, down_weight):
    vmem = pl.BlockSpec(memory_space=pltpu.VMEM)
    hbm = pl.BlockSpec(memory_space=pl.ANY)
    bf16, f32, i16 = jnp.bfloat16, jnp.float32, jnp.int16
    dma = pltpu.SemaphoreType.DMA
    return pl.pallas_call(
        kernel,
        out_shape=jax.ShapeDtypeStruct((FEAT, FEAT), bf16),
        in_specs=[vmem] * 5 + [hbm] * 3,
        out_specs=vmem,
        scratch_shapes=[
            pltpu.VMEM((HID, WIDTH), bf16),
            pltpu.VMEM((HID, WIDTH), bf16),
            pltpu.VMEM((2, SIDE, HID, SIDE * FEAT), bf16),
            pltpu.VMEM((ROWS, FEAT), bf16),
            pltpu.VMEM((2, 16, ROWS, FEAT), bf16),
            pltpu.VMEM((ROWS, FEAT), f32),
            pltpu.VMEM((1, ROWS), f32),
            pltpu.VMEM((ZS, 1, ROWS), f32),
            pltpu.VMEM((FEAT, FEAT), f32),
            pltpu.VMEM((10, 1, FEAT), f32),
            pltpu.VMEM((2, ROWS, 2 * FEAT), bf16),
            pltpu.VMEM((ROWS, HID), f32),
            pltpu.VMEM((ROWS, HID), f32),
            pltpu.VMEM((2, ROWS, HID), bf16),
            pltpu.VMEM((SIDE, ROWS, SIDE * FEAT), f32),
            pltpu.VMEM((2, HALF, FEAT), f32),
            pltpu.VMEM((2, SIDE, QROWS, FEAT), i16),
            pltpu.VMEM((2, SIDE, 2, QROWS, FEAT), i16),
            pltpu.VMEM((2, SIDE, QROWS, FEAT), i16),
            pltpu.VMEM((2, SIDE, 2, QROWS, FEAT), i16),
            pltpu.VMEM((2, QROWS, FEAT), i16),
            pltpu.VMEM((2, 2, QROWS, FEAT), i16),
            pltpu.VMEM((2, QROWS, FEAT), i16),
            pltpu.VMEM((2, 2, QROWS, FEAT), i16),
            pltpu.VMEM((ROWS, FEAT), bf16),
            pltpu.VMEM((ROWS, FEAT), bf16),
            dma((2,)), dma, dma, dma,
            dma((ZS - 1,)), dma((ZS - 1,)), dma((ZS - 1,)), dma((ZS - 1,)),
            dma((7,)), dma((7,)),
            dma((30,)), dma((32,)), dma((16,)), dma((16,)), dma((4,)), dma((4,)),
            dma((3, 2, SIDE)), dma((2, SIDE)), dma((2, SIDE, 2)),
            dma((3, 2)), dma((2,)), dma((2, 2)),
            dma((ZS - 1,)), dma((ZS - 1,)),
        ],
        compiler_params=pltpu.CompilerParams(collective_id=0, has_side_effects=True, vmem_limit_bytes=60 * 1024 * 1024),
    )(
        tokens,
        norm_gain.reshape(16, 1, 2 * FEAT),
        route_logits.T,
        expert_ids.T,
        active.reshape(1, FEAT),
        gate_weight.reshape(HID, WIDTH),
        up_weight.reshape(HID, WIDTH),
        down_weight.reshape(HID, WIDTH),
    )


def solution(mesh):
    split = Mesh(mesh.devices.reshape(ZS, SIDE, SIDE, 2), ("expert", "x", "y", "c"))
    plane = ("x", "y", "c")
    weight = P("expert", plane, None)
    in_specs = (P("expert", plane), P(), P("expert", None), P("expert", None), P("expert"), weight, weight, weight)
    return jax.shard_map(local, mesh=split, in_specs=in_specs, out_specs=P("expert", plane), check_vma=False)
```

time: 244 us -> 65.7 us (0.27)
  waiting for transfers between devices: 155 us -> 0 us
  Pallas kernels: 0 us -> 62.7 us
  blocking collectives: 39.4 us -> 0 us
  matrix products: 19.3 us -> 0 us
  between operations: 13.5 us -> 0.01 us
  starting transfers between devices: 7.11 us -> 0 us
  other arithmetic: 5.48 us -> 0 us
    reduce_scatter x1 -> x0, waiting for transfers between devices: 99.5 us -> none  [own_rows(): own = lax.psum_scatter(everything, axis, scatter_dimension=0, tiled=True)]
    pallas_call x0 -> x1, Pallas kernels: none -> 62.7 us  [local(): pl.pallas_call(kernel, out_shape=jax.ShapeDtypeStruct((FEAT, FEAT), bf16)...]
    all_gather x1 -> x0, waiting for transfers between devices: 46.9 us -> none  [taken_in(): lax.all_gather(a, axis, axis=dim, tiled=True)]
    psum x3 -> x0, blocking collectives: 21.8 us -> none  [one_axis_at_a_time(): shard = lax.psum(shard, axis)]
    dot_general x4 -> x0, matrix products: 19.3 us -> none  [the longest x1 12 us: down_terms(): jnp.einsum('hzj,hjs->shz', inner_width, lowering_share, preferred_element...]
    all_to_all x1 -> x0, blocking collectives: 17.6 us -> none  [local(): lax.all_to_all(send_rows, 'expert', split_axis=0, concat_axis=0, tiled=True)]
    all_to_all x1 -> x0, waiting for transfers between devices: 8.7 us -> none  [local(): lax.all_to_all(returning, 'expert', split_axis=0, concat_axis=0, tiled=True)]
    all_to_all x1 -> x0, starting transfers between devices: 7.07 us -> none  [local(): lax.all_to_all(returning, 'expert', split_axis=0, concat_axis=0, tiled=True)]
  transfers between devices with their start and end apart: 3 -> 0, of which waited for: 3 -> 0; matrix products, arithmetic and copies ran while one was open for 0% -> 0% of each run, Pallas kernels for 0% -> 0%
where the time goes in v1:
time: 65.7 us; the launch traced here: 65.4 us
  Pallas kernels  62.7 us (95%)
  local copies, waits for them, and re-layouts  2.69 us (4%)
    pallas_call x1, Pallas kernels, local(): pl.pallas_call(kernel, out_shape=jax.ShapeDtypeStruct((FEAT, FEAT), bf16)...  62.7 us
    unnamed x1, local copies, waits for them, and re-layouts  1.38 us

profile of v1, /device:TPU:2, one launch (start us, length us, event | category | flops | bytes accessed | tf_op | source)
XLA Modules:
  0.0 65.4 jit_solution(1460805177280386334)
XLA Ops:
  0.0 1.3 %reshape.20.gain_ref = bf16[16,1,256]{2,1,0:T(2,128)(2,1)} reshape(bf16[4096]{0:T(1024)(128)(2,1)} %param.9) | data formatting | bytes 16384 | tf_op jit(solution)/shard_map/reshape | solution.py:395
  1.3 62.7 %shard_map.82 = bf16[128,128]{1,0:T(8,128)(2,1)} custom-call(bf16[128,128]{1,0:T(8,128)(2,1)} %tok_ref.1, bf16[16,1,256]{2,1,0:T(2,128)(2,1)} %reshape.20.gain_ref, f32[2,128]{1,0:T(2,128)} %bitcast.9, s32[2,128]{1,0:T(2,128)} %bitcast.10, s32[1,128]{1,0:T(1,128)} %bitcast.11, bf16[448,4096]{1,0:T(8,128)(2,1)} %bitcast.6, bf16[448,4096]{1,0:T(8,128)(2,1)} %bitcast.7, ...), custom_call_target="tpu_custom_call" | custom-call | tf_op jit(solution)/shard_map/pallas_call | solution.py:352
  64.0 1.4 %copy.11 = bf16[128,128]{1,0:T(8,128)(2,1)} copy(bf16[128,128]{1,0:T(8,128)(2,1)} %shard_map.82) | data formatting | bytes 65536

commit v2 on v0

v2 whole, which is shorter than its diff:
```python
import jax
import jax.numpy as jnp
from jax import lax
from jax.experimental import pallas as pl
from jax.experimental.pallas import tpu as pltpu
from jax.sharding import Mesh
from jax.sharding import PartitionSpec as P

MESH = pl.DeviceIdType.MESH
EPS = 1e-05
ZS = 8
SIDE = 4
SEATS = 64
ROWS = ZS * SEATS
HALF = ROWS // 2
QUARTER = HALF // 2
FEAT = 128
HID = 448
WIDTH = 4096
QMAX = 32000.0

ORDER = [(0, 0), (3, 0), (1, 0), (0, 3), (0, 1), (2, 0), (3, 3), (3, 1), (1, 3), (1, 1), (0, 2), (2, 3), (2, 1), (3, 2), (1, 2), (2, 2)]
MIRROR = [ORDER.index((j, i)) for i, j in ORDER]
PRODUCTS = ((1, 3), (2, 4), (5, 10), (0, 6), (7, 8), (9, 11), (13, 12), (14, 15))
BLOCKS = ((2, 3), (1, 0))

SCHEDULE = (
    ("arr", 0, 1), ("arr", 0, 2), ("arr", 0, 3), ("arr", 0, 4), ("arr", 1, 3), ("arr", 1, 4),
    ("arr", 1, 1), ("arr", 1, 2), ("arr", 0, 5), ("scale", 0), ("weights",), ("prod", 0, 0),
    ("scale", 1), ("arr", 0, 6), ("arr", 0, 7), ("prod", 0, 1), ("arr", 1, 5), ("prod", 1, 0),
    ("arr", 0, 8), ("arr", 0, 9), ("arr", 0, 10), ("prod", 1, 1), ("arr", 1, 10), ("prod", 0, 3),
    ("arr", 1, 6), ("arr", 1, 7), ("prod", 0, 4), ("prod", 0, 2), ("arr", 1, 8), ("arr", 1, 9),
    ("prod", 1, 2), ("arr", 0, 11), ("arr", 0, 12), ("prod", 1, 3), ("arr", 0, 13), ("prod", 1, 4),
    ("arr", 1, 11), ("arr", 1, 12), ("arr", 0, 14), ("arr", 1, 13), ("prod", 0, 5), ("arr", 1, 14),
    ("prod", 0, 6), ("arr", 0, 15), ("prod", 1, 5), ("prod", 1, 6), ("arr", 1, 15), ("prod", 0, 7),
    ("hidden", 0), ("down",), ("pre2", 0), ("prod", 1, 7), ("hidden", 1), ("pre2", 1),
    ("p2", 0), ("ahead", 0, 0), ("ahead", 0, 1), ("pd", 0, 0), ("direct", 0, 0, 0), ("direct", 0, 1, 0),
    ("pd", 0, 1), ("direct", 0, 0, 1), ("direct", 0, 1, 1), ("p2", 1), ("ahead", 1, 0), ("ahead", 1, 1),
    ("pd", 1, 0), ("direct", 1, 0, 0), ("direct", 1, 1, 0), ("pd", 1, 1), ("direct", 1, 0, 1), ("direct", 1, 1, 1),
    ("p0", 0), ("joined", 0, 0, 0), ("joined", 0, 0, 1), ("p0", 1), ("joined", 0, 1, 0), ("joined", 0, 1, 1),
    ("joined", 1, 0, 0), ("joined", 1, 0, 1), ("joined", 1, 1, 0), ("joined", 1, 1, 1), ("sum", 0, 0), ("sum", 0, 2),
    ("sum", 0, 1), ("own", 0), ("sum", 1, 0), ("sum", 1, 2), ("sum", 1, 1), ("own", 1),
    ("finish", 0), ("finish", 1),
)


def encode(values, ref):
    row = lax.broadcasted_iota(jnp.int32, (16, FEAT), 0)
    scale = jnp.zeros((16, FEAT), jnp.int32)
    for n, v in enumerate(values):
        top = jnp.maximum(jnp.max(jnp.abs(v), axis=0, keepdims=True), 1e-30)
        exponent = jnp.ceil(jnp.log2(top))
        power = jnp.exp2(exponent)
        mantissa = jnp.ceil(top / power * QMAX)
        inverse = (QMAX * QMAX) / (mantissa * power)
        ref[n * QUARTER : (n + 1) * QUARTER, :] = jnp.round(v * inverse).astype(jnp.int32).astype(jnp.int16)
        scale = jnp.where(row >= 8 * n, jnp.where(row < 8 * n + 4, exponent.astype(jnp.int32), mantissa.astype(jnp.int32)), scale)
    ref[len(values) * QUARTER :, :] = scale.astype(jnp.int16)


def decode(ref, n=0):
    scale = ref[ref.shape[0] - 16 :, :].astype(jnp.int32).astype(jnp.float32)
    factor = scale[8 * n + 4 : 8 * n + 5, :] * jnp.exp2(scale[8 * n : 8 * n + 1, :]) * (1.0 / (QMAX * QMAX))
    return ref[n * QUARTER : (n + 1) * QUARTER, :].astype(jnp.int32).astype(jnp.float32) * factor


def column(row):
    return jnp.broadcast_to(row, (FEAT, FEAT)).T


def dot(a, b, dims, precision=None):
    return lax.dot_general(a, b, (dims, ((), ())), precision=precision, preferred_element_type=jnp.float32)


def kernel(
    tok_ref, gain_ref, logit_ref, ids_ref, act_ref, wg_hbm, wu_hbm, wd_hbm, out_ref,
    wide_w, dn, outbox, gathered, scale_rows, rsend, rrecv, turned, msb, xn, sums, hid, part, red,
    sfb, sdb, rfb, rdb, sda, rda, fin, ret,
    w_sem, dn_sem, dns_sem, dnr_sem, z_s, z_r, rz_s, rz_r, ms_s, ms_r, g_s, g_r, d_s, d_r, h_s, h_r,
    bf_s, bf_r, bd_s, bd_r, ad_s, ad_r, t_s, t_r,
):
    z, x, y, c = (lax.axis_index(n) for n in ("expert", "x", "y", "c"))
    a = jnp.where(c == 0, x, y)
    b = jnp.where(c == 0, y, x)
    mate = {"c": 1 - c}

    def wrap(v):
        return lax.rem(v, SIDE)

    def to_a(s):
        return {"x": wrap(x + s * (1 - c)), "y": wrap(y + s * c)}

    def to_b(s):
        return {"x": wrap(x + s * c), "y": wrap(y + s * (1 - c))}

    def to_z(s):
        return {"expert": lax.rem(z + s, ZS)}

    def remote(src, dst, s_sem, r_sem, device):
        pltpu.make_async_remote_copy(src_ref=src, dst_ref=dst, send_sem=s_sem, recv_sem=r_sem, device_id=device, device_id_type=MESH).start()

    def arrived(ref, sem):
        pltpu.make_async_copy(ref, ref, sem).wait()

    for n, w in enumerate((wg_hbm, wu_hbm)):
        pltpu.make_async_copy(w, wide_w.at[n], w_sem).start()

    def down_columns(aa, bb, core):
        xx = jnp.where(core == 0, aa, bb)
        yy = jnp.where(core == 0, bb, aa)
        return pl.ds(pl.multiple_of(((xx * SIDE + yy) * 2 + core) * FEAT, FEAT), FEAT)

    barrier = pltpu.get_barrier_semaphore()
    peers = [mate] + [{"x": wrap(x + s)} for s in (1, 2, 3)] + [{"y": wrap(y + s)} for s in (1, 2, 3)] + [to_z(s) for s in range(1, ZS)]
    for peer in peers:
        pl.semaphore_signal(barrier, inc=1, device_id=peer, device_id_type=MESH)

    for aa in range(SIDE):
        for bb in range(SIDE):
            pltpu.make_async_copy(wd_hbm.at[:, down_columns(aa, bb, c)], dn.at[c, bb, :, pl.ds(aa * FEAT, FEAT)], dn_sem).start()

    tok = tok_ref[...]
    wide = tok.astype(jnp.float32)
    msb[0] = jnp.sum((wide * wide).T, axis=0, keepdims=True)

    seat_row = lax.broadcasted_iota(jnp.int32, (ROWS, FEAT), 0)
    expert_of = seat_row // SEATS
    seat_of = (seat_row - expert_of * SEATS).astype(jnp.float32)
    live = jnp.broadcast_to(act_ref[...], (ROWS, FEAT)) > 0
    first = (expert_of == jnp.broadcast_to(ids_ref[0:1, :], (ROWS, FEAT))) & live
    second = (expert_of == jnp.broadcast_to(ids_ref[1:2, :], (ROWS, FEAT))) & live
    named = jnp.where(first | second, 1.0, 0.0)
    before = jnp.where(lax.broadcasted_iota(jnp.int32, (FEAT, FEAT), 0) < lax.broadcasted_iota(jnp.int32, (FEAT, FEAT), 1), 1.0, 0.0)
    position = dot(named.astype(jnp.bfloat16), before.astype(jnp.bfloat16), ((1,), (0,)))
    seated = position == seat_of
    pick0 = jnp.where(first & seated, 1.0, 0.0)
    pick1 = jnp.where(second & seated, 1.0, 0.0)
    pick = (pick0 + pick1).astype(jnp.bfloat16)
    outbox[...] = dot(pick, tok, ((1,), (0,))).astype(jnp.bfloat16)

    pl.semaphore_wait(barrier, len(peers))
    remote(msb.at[0], msb.at[1], ms_s, ms_r.at[0], mate)
    me = a * SIDE + b
    my_half = z // 4
    own_seats = pl.ds(pl.multiple_of(z * SEATS, SEATS), SEATS)
    landing = gathered.at[my_half, c, me, pl.ds(pl.multiple_of(z % 4 * SEATS, SEATS), SEATS)]
    for s in (4, 5, 3, 6, 2, 7, 1):
        target = lax.rem(z + s, ZS)
        remote(outbox.at[pl.ds(pl.multiple_of(target * SEATS, SEATS), SEATS)], landing, z_s, z_r.at[my_half], to_z(s))
    pltpu.make_async_copy(outbox.at[own_seats], landing, z_r.at[my_half]).start()
    for aa in range(SIDE):
        for bb in range(SIDE):
            remote(wd_hbm.at[:, down_columns(aa, bb, 1 - c)], dn.at[c, bb, :, pl.ds(aa * FEAT, FEAT)], dns_sem, dnr_sem, mate)

    def pass_on(h, i, j, quarter, device, di, dj):
        k = wrap(a + i) * SIDE + wrap(b + j)
        ref = gathered.at[h, c, k]
        if quarter is not None:
            ref = ref.at[pl.ds(quarter * QUARTER, QUARTER)]
        remote(ref, ref, g_s, g_r.at[h, ORDER.index(((i - di) % 4, (j - dj) % 4))], device)

    def arrive(h, n):
        i, j = ORDER[n]
        k = wrap(a + i) * SIDE + wrap(b + j)
        if n == 0:
            arrived(gathered.at[h, c, k], z_r.at[h])
            pass_on(h, 0, 0, None, to_a(1), 1, 0)
            pass_on(h, 0, 0, None, to_a(3), 3, 0)
            pass_on(h, 0, 0, None, to_a(2), 2, 0)
        else:
            arrived(gathered.at[h, c, k], g_r.at[h, n])
        if j == 0:
            pass_on(h, i, j, None, to_b(1), 0, 1)
            pass_on(h, i, j, None, to_b(3), 0, 3)
        if j == 3:
            pass_on(h, i, j, 0, to_b(1), 0, 1)
        if j == 1:
            pass_on(h, i, j, 1, to_b(3), 0, 3)
        group = next(g for g, pair in enumerate(PRODUCTS) if MIRROR[n] in pair)
        remote(gathered.at[h, c, k], gathered.at[h, c, k], d_s, d_r.at[h, group], mate)

    opened = set()

    def product(h, group):
        arrived(gathered.at[h, 0, pl.ds(0, 2)], d_r.at[h, group])
        offsets = []
        for p, n in enumerate(PRODUCTS[group]):
            i, j = ORDER[n]
            aa, bb = wrap(a + i), wrap(b + j)
            mine, other = aa * SIDE + bb, bb * SIDE + aa
            chip = jnp.where(c == 0, mine, other)
            at = pl.ds(pl.multiple_of(chip * 2 * FEAT, 2 * FEAT), 2 * FEAT)
            gains = gain_ref[at].astype(jnp.float32).reshape(1, 2 * FEAT)
            for core in (0, 1):
                k = jnp.where(c == core, mine, other)
                lanes = slice(core * FEAT, (core + 1) * FEAT)
                normed = gathered[h, core, k].astype(jnp.float32) * scale_rows[h] * gains[:, lanes]
                xn[p, :, lanes] = normed.astype(jnp.bfloat16)
            offsets.append(at)
        for n in (0, 1):
            terms = sum(dot(xn[p], wide_w[n, :, at], ((1,), (1,))) for p, at in enumerate(offsets))
            sums[h, n] = sums[h, n] + terms if h in opened else terms
        opened.add(h)

    def hidden(h):
        g = sums[h, 0]
        hid[h, c] = (g / (1.0 + jnp.exp(-g)) * sums[h, 1]).astype(jnp.bfloat16)
        remote(hid.at[h, c], hid.at[h, c], h_s, h_r.at[h], mate)

    AHEAD, STEP, SIDES = 2, (1, 3), (1, 3)

    def partial(h, j, own, first):
        core = c if own else 1 - c
        terms = dot(hid[h, core], dn[core, wrap(b + j)], ((1,), (0,)))
        part[h, j] = terms if first else part[h, j] + terms

    def block(h, j, q, i):
        return part[h, j, q * QUARTER : (q + 1) * QUARTER, pl.ds(pl.multiple_of(wrap(a + i) * FEAT, FEAT), FEAT)]

    def send_ahead(h, g):
        for d in (0, 1):
            encode([block(h, AHEAD, d, i) for i in BLOCKS[g]], sfb.at[h, d, g])
            remote(sfb.at[h, d, g], rfb.at[h, d, g], bf_s, bf_r.at[h, d, g], to_b(STEP[d]))

    def send_direct(h, g, d):
        q = 1 - d
        encode([block(h, SIDES[d], q, i) for i in BLOCKS[g]], sdb.at[h, g, d, q])
        remote(sdb.at[h, g, d, q], rdb.at[h, g, d, q], bd_s, bd_r.at[h, g], to_b(STEP[d]))

    def send_joined(h, g, d):
        q = d
        arrived(rfb.at[h, d, g], bf_r.at[h, d, g])
        encode([block(h, SIDES[d], q, i) + decode(rfb.at[h, d, g], n) for n, i in enumerate(BLOCKS[g])], sdb.at[h, g, d, q])
        remote(sdb.at[h, g, d, q], rdb.at[h, g, d, q], bd_s, bd_r.at[h, g], to_b(STEP[d]))

    awaited = set()

    def summed(h, i):
        g = 0 if i in BLOCKS[0] else 1
        n = BLOCKS[g].index(i)
        if (h, g) not in awaited:
            awaited.add((h, g))
            arrived(rdb.at[h, g], bd_r.at[h, g])
        return [block(h, 0, q, i) + decode(rdb.at[h, g, 0, q], n) + decode(rdb.at[h, g, 1, q], n) for q in (0, 1)]

    def send_sum(h, n):
        i = (2, 1, 3)[n]
        encode(summed(h, i), sda.at[h, n])
        remote(sda.at[h, n], rda.at[h, n], ad_s, ad_r.at[h], to_a(i))

    def keep_sum(h):
        red[h, 0], red[h, 1] = summed(h, 0)

    def finish(h):
        arrived(rda.at[h], ad_r.at[h])
        for q in (0, 1):
            total = red[h, q] + decode(rda.at[h, 0], q) + decode(rda.at[h, 1], q) + decode(rda.at[h, 2], q)
            fin[h, q * QUARTER : (q + 1) * QUARTER, :] = total.astype(jnp.bfloat16)
        for m in range(4):
            g = h * 4 + m
            source, target = fin.at[h, pl.ds(m * SEATS, SEATS)], ret.at[own_seats]

            @pl.when(z != g)
            def _():
                remote(source, target, t_s, t_r, {"expert": g})

            @pl.when(z == g)
            def _():
                pltpu.make_async_copy(source, target, t_r).start()

    arrived(msb.at[1], ms_r.at[0])
    msb[2] = msb[0] + msb[1]
    for s in (1, 2, 3):
        remote(msb.at[2], msb.at[2 + s], ms_s, ms_r.at[1], {"x": wrap(x + s)})
    arrived(msb.at[pl.ds(3, 3)], ms_r.at[1])
    msb[6] = (msb[2] + msb[3]) + (msb[4] + msb[5])
    for s in (1, 2, 3):
        remote(msb.at[6], msb.at[6 + s], ms_s, ms_r.at[2], {"y": wrap(y + s)})
    arrive(0, 0)
    arrive(1, 0)
    arrived(msb.at[pl.ds(7, 3)], ms_r.at[2])
    mean_square = ((msb[6] + msb[7]) + (msb[8] + msb[9])) / WIDTH
    inverse = lax.rsqrt(mean_square + EPS)
    rsend[...] = dot(jnp.broadcast_to(inverse, (8, FEAT)), pick.astype(jnp.float32), ((1,), (1,)), lax.Precision.HIGHEST)[0:1, :]
    for s in range(1, ZS):
        remote(rsend, rrecv.at[z], rz_s, rz_r.at[my_half], to_z(s))
    pltpu.make_async_copy(rsend, rrecv.at[z], rz_r.at[my_half]).start()
    l0, l1 = logit_ref[0:1, :], logit_ref[1:2, :]
    high = jnp.maximum(l0, l1)
    e0, e1 = jnp.exp(l0 - high), jnp.exp(l1 - high)
    alive = act_ref[...].astype(jnp.float32)
    prob0 = column(e0 / (e0 + e1) * alive)
    prob1 = column(e1 / (e0 + e1) * alive)

    lane_block = pl.ds(pl.multiple_of(z // 2 * FEAT, FEAT), FEAT)
    seat_block = pl.ds(pl.multiple_of(z % 2 * SEATS, SEATS), SEATS)

    def scales(h):
        arrived(rrecv.at[pl.ds(0, 4)], rz_r.at[h])
        for m in range(4):
            turned[...] = column(rrecv[h * 4 + m, :, lane_block])
            scale_rows[h, m * SEATS : (m + 1) * SEATS, :] = turned[seat_block, :]

    def down_ready():
        arrived(dn.at[c], dn_sem)
        arrived(dn.at[1 - c], dnr_sem)

    def weights_ready():
        arrived(wide_w, w_sem)

    def both_cores(h):
        arrived(hid.at[h, 1 - c], h_r.at[h])
        partial(h, AHEAD, False, False)

    def whole_partial(h, j):
        partial(h, j, True, True)
        partial(h, j, False, False)

    events = {
        "arr": arrive,
        "scale": scales,
        "weights": weights_ready,
        "prod": product,
        "hidden": hidden,
        "down": down_ready,
        "pre2": lambda h: partial(h, AHEAD, True, True),
        "p2": both_cores,
        "ahead": send_ahead,
        "pd": lambda h, d: whole_partial(h, SIDES[d]),
        "direct": send_direct,
        "joined": send_joined,
        "p0": lambda h: whole_partial(h, 0),
        "sum": send_sum,
        "own": keep_sum,
        "finish": finish,
    }
    for name, *which in SCHEDULE:
        events[name](*which)
    arrived(ret, t_r)
    back = ret[...]
    from0 = dot(pick0.astype(jnp.bfloat16), back, ((0,), (0,)))
    from1 = dot(pick1.astype(jnp.bfloat16), back, ((0,), (0,)))
    out_ref[...] = (prob0 * from0 + prob1 * from1).astype(jnp.bfloat16)

    arrived(outbox.at[pl.ds(0, ROWS - SEATS)], z_s)
    arrived(rrecv.at[pl.ds(0, ZS - 1)], rz_s)
    arrived(msb.at[pl.ds(0, 7)], ms_s)
    arrived(gathered.at[:, 0, pl.ds(0, 15)], g_s)
    arrived(gathered.at[:, 0], d_s)
    arrived(hid.at[:, 0], h_s)
    arrived(sfb, bf_s)
    arrived(sdb, bd_s)
    arrived(sda, ad_s)
    arrived(ret.at[pl.ds(0, ROWS - SEATS)], t_s)
    arrived(dn.at[c], dns_sem)


def local(tokens, norm_gain, route_logits, expert_ids, active, gate_weight, up_weight, down_weight):
    vmem = pl.BlockSpec(memory_space=pltpu.VMEM)
    hbm = pl.BlockSpec(memory_space=pltpu.HBM)
    bf16, f32, i16 = jnp.bfloat16, jnp.float32, jnp.int16
    dma = pltpu.SemaphoreType.DMA
    double = 2 * QUARTER + 16
    return pl.pallas_call(
        kernel,
        out_shape=jax.ShapeDtypeStruct((FEAT, FEAT), bf16),
        in_specs=[vmem] * 5 + [hbm] * 3,
        out_specs=vmem,
        scratch_shapes=[
            pltpu.VMEM((2, HID, WIDTH), bf16),
            pltpu.VMEM((2, SIDE, HID, SIDE * FEAT), bf16),
            pltpu.VMEM((ROWS, FEAT), bf16),
            pltpu.VMEM((2, 2, 16, HALF, FEAT), bf16),
            pltpu.VMEM((2, HALF, FEAT), f32),
            pltpu.VMEM((1, ROWS), f32),
            pltpu.VMEM((ZS, 1, ROWS), f32),
            pltpu.VMEM((FEAT, FEAT), f32),
            pltpu.VMEM((10, 1, FEAT), f32),
            pltpu.VMEM((2, HALF, 2 * FEAT), bf16),
            pltpu.VMEM((2, 2, HALF, HID), f32),
            pltpu.VMEM((2, 2, HALF, HID), bf16),
            pltpu.VMEM((2, SIDE, HALF, SIDE * FEAT), f32),
            pltpu.VMEM((2, 2, QUARTER, FEAT), f32),
            pltpu.VMEM((2, 2, 2, double, FEAT), i16),
            pltpu.VMEM((2, 2, 2, 2, double, FEAT), i16),
            pltpu.VMEM((2, 2, 2, double, FEAT), i16),
            pltpu.VMEM((2, 2, 2, 2, double, FEAT), i16),
            pltpu.VMEM((2, 3, double, FEAT), i16),
            pltpu.VMEM((2, 3, double, FEAT), i16),
            pltpu.VMEM((2, HALF, FEAT), bf16),
            pltpu.VMEM((ROWS, FEAT), bf16),
            dma, dma, dma, dma,
            dma, dma((2,)), dma, dma((2,)), dma, dma((3,)),
            dma, dma((2, 16)), dma, dma((2, 8)), dma, dma((2,)),
            dma, dma((2, 2, 2)), dma, dma((2, 2)), dma, dma((2,)),
            dma, dma,
        ],
        compiler_params=pltpu.CompilerParams(collective_id=0, has_side_effects=True, vmem_limit_bytes=52 * 1024 * 1024),
    )(
        tokens,
        norm_gain,
        route_logits.T,
        expert_ids.T,
        active.reshape(1, FEAT),
        gate_weight.reshape(HID, WIDTH),
        up_weight.reshape(HID, WIDTH),
        down_weight.reshape(HID, WIDTH),
    )


def solution(mesh):
    split = Mesh(mesh.devices.reshape(ZS, SIDE, SIDE, 2), ("expert", "x", "y", "c"))
    plane = ("x", "y", "c")
    weight = P("expert", plane, None)
    in_specs = (P("expert", plane), P(), P("expert", None), P("expert", None), P("expert"), weight, weight, weight)
    return jax.shard_map(local, mesh=split, in_specs=in_specs, out_specs=P("expert", plane), check_vma=False)
```

time: 244 us -> 58.5 us (0.24)
  the two profiles are of different devices: /device:TPU:2 before, /device:TPU:1 now
where the time goes in v2:
time: 58.5 us; the launch traced here: 58.3 us
  Pallas kernels  54.2 us (93%)
  local copies, waits for them, and re-layouts  4.08 us (7%)
    pallas_call x1, Pallas kernels, local(): pl.pallas_call(kernel, out_shape=jax.ShapeDtypeStruct((FEAT, FEAT), bf16)...  54.2 us
    unnamed x11, local copies, waits for them, and re-layouts  4.08 us

profile of v2, /device:TPU:1, one launch (start us, length us, event | category | flops | bytes accessed | tf_op | source)
XLA Modules:
  0.0 58.3 jit_solution(17492196406956107801)
XLA Ops:
  0.0 0.0 copy-start
  0.0 0.8 %copy-done = bf16[128,128]{1,0:T(8,128)(2,1)S(1)} copy-done((bf16[128,128]{1,0:T(8,128)(2,1)S(1)}, bf16[128,128]{1,0:T(8,128)(2,1)}, u32[]{:S(2)}) %copy-start) | copy-done | bytes 32792
  0.8 0.0 copy-start.1
  0.8 0.7 %copy-done.1 = bf16[4096]{0:T(1024)(128)(2,1)S(1)} copy-done((bf16[4096]{0:T(1024)(128)(2,1)S(1)}, bf16[4096]{0:T(1024)(128)(2,1)}, u32[]{:S(2)}) %copy-start.1) | copy-done | bytes 8216
  1.5 0.0 copy-start.2
  1.5 0.7 %copy-done.2 = f32[128,2]{0,1:T(2,128)S(1)} copy-done((f32[128,2]{0,1:T(2,128)S(1)}, f32[128,2]{0,1:T(2,128)}, u32[]{:S(2)}) %copy-start.2) | copy-done | bytes 1048
  2.1 0.0 copy-start.3
  2.1 0.7 %copy-done.3 = s32[128,2]{0,1:T(2,128)S(1)} copy-done((s32[128,2]{0,1:T(2,128)S(1)}, s32[128,2]{0,1:T(2,128)}, u32[]{:S(2)}) %copy-start.3) | copy-done | bytes 1048
  2.8 0.0 copy-start.4
  2.8 0.7 %copy-done.4 = s32[128]{0:T(128)S(1)} copy-done((s32[128]{0:T(128)S(1)}, s32[128]{0:T(128)}, u32[]{:S(2)}) %copy-start.4) | copy-done | bytes 536
  3.5 54.2 %shard_map.82 = bf16[128,128]{1,0:T(8,128)(2,1)S(1)} custom-call(bf16[128,128]{1,0:T(8,128)(2,1)S(1)} %copy-done, bf16[4096]{0:T(1024)(128)(2,1)S(1)} %copy-done.1, f32[2,128]{1,0:T(2,128)S(1)} %bitcast.6, s32[2,128]{1,0:T(2,128)S(1)} %bitcast.7, s32[1,128]{1,0:T(1,128)S(1)} %bitcast.8, bf16[448,4096]{1,0:T(8,128)(2,1)} %bitcast.9, ...), custom_call_target="tpu_custom_call" | custom-call | tf_op jit(solution)/shard_map/pallas_call | solution.py:364
  57.7 0.6 %copy.10 = bf16[128,128]{1,0:T(8,128)(2,1)} copy(bf16[128,128]{1,0:T(8,128)(2,1)S(1)} %shard_map.82) | data formatting | bytes 65536
Async XLA Ops:
  0.0 0.8 %copy-start = (bf16[128,128]{1,0:T(8,128)(2,1)S(1)}, bf16[128,128]{1,0:T(8,128)(2,1)}, u32[]{:S(2)}) copy-start(bf16[128,128]{1,0:T(8,128)(2,1)} %tok_ref.1) | copy-start | bytes 98308
  0.8 0.7 %copy-start.1 = (bf16[4096]{0:T(1024)(128)(2,1)S(1)}, bf16[4096]{0:T(1024)(128)(2,1)}, u32[]{:S(2)}) copy-start(bf16[4096]{0:T(1024)(128)(2,1)} %gain_ref.1) | copy-start | bytes 24580
  1.5 0.7 %copy-start.2 = (f32[128,2]{0,1:T(2,128)S(1)}, f32[128,2]{0,1:T(2,128)}, u32[]{:S(2)}) copy-start(f32[128,2]{0,1:T(2,128)} %param.10) | copy-start | bytes 3076
  2.1 0.7 %copy-start.3 = (s32[128,2]{0,1:T(2,128)S(1)}, s32[128,2]{0,1:T(2,128)}, u32[]{:S(2)}) copy-start(s32[128,2]{0,1:T(2,128)} %param.11) | copy-start | bytes 3076
  2.8 0.7 %copy-start.4 = (s32[128]{0:T(128)S(1)}, s32[128]{0:T(128)}, u32[]{:S(2)}) copy-start(s32[128]{0:T(128)} %param.12) | copy-start | bytes 1540

commit v3 on v2

--- a/solution.py
+++ b/solution.py
@@ -25,22 +25,22 @@
 BLOCKS = ((2, 3), (1, 0))
 
 SCHEDULE = (
-    ("arr", 0, 1), ("arr", 0, 2), ("arr", 0, 3), ("arr", 0, 4), ("arr", 1, 3), ("arr", 1, 4),
-    ("arr", 1, 1), ("arr", 1, 2), ("arr", 0, 5), ("scale", 0), ("weights",), ("prod", 0, 0),
-    ("scale", 1), ("arr", 0, 6), ("arr", 0, 7), ("prod", 0, 1), ("arr", 1, 5), ("prod", 1, 0),
-    ("arr", 0, 8), ("arr", 0, 9), ("arr", 0, 10), ("prod", 1, 1), ("arr", 1, 10), ("prod", 0, 3),
-    ("arr", 1, 6), ("arr", 1, 7), ("prod", 0, 4), ("prod", 0, 2), ("arr", 1, 8), ("arr", 1, 9),
-    ("prod", 1, 2), ("arr", 0, 11), ("arr", 0, 12), ("prod", 1, 3), ("arr", 0, 13), ("prod", 1, 4),
-    ("arr", 1, 11), ("arr", 1, 12), ("arr", 0, 14), ("arr", 1, 13), ("prod", 0, 5), ("arr", 1, 14),
-    ("prod", 0, 6), ("arr", 0, 15), ("prod", 1, 5), ("prod", 1, 6), ("arr", 1, 15), ("prod", 0, 7),
-    ("hidden", 0), ("down",), ("pre2", 0), ("prod", 1, 7), ("hidden", 1), ("pre2", 1),
-    ("p2", 0), ("ahead", 0, 0), ("ahead", 0, 1), ("pd", 0, 0), ("direct", 0, 0, 0), ("direct", 0, 1, 0),
-    ("pd", 0, 1), ("direct", 0, 0, 1), ("direct", 0, 1, 1), ("p2", 1), ("ahead", 1, 0), ("ahead", 1, 1),
-    ("pd", 1, 0), ("direct", 1, 0, 0), ("direct", 1, 1, 0), ("pd", 1, 1), ("direct", 1, 0, 1), ("direct", 1, 1, 1),
-    ("p0", 0), ("joined", 0, 0, 0), ("joined", 0, 0, 1), ("p0", 1), ("joined", 0, 1, 0), ("joined", 0, 1, 1),
-    ("joined", 1, 0, 0), ("joined", 1, 0, 1), ("joined", 1, 1, 0), ("joined", 1, 1, 1), ("sum", 0, 0), ("sum", 0, 2),
-    ("sum", 0, 1), ("own", 0), ("sum", 1, 0), ("sum", 1, 2), ("sum", 1, 1), ("own", 1),
-    ("finish", 0), ("finish", 1),
+    ("arr", 0, 1), ("arr", 0, 2), ("arr", 0, 3), ("arr", 1, 4), ("arr", 1, 3), ("arr", 0, 4),
+    ("arr", 1, 1), ("scale", 0), ("arr", 0, 5), ("arr", 1, 2), ("scale", 1), ("weights",),
+    ("prod", 1, 1), ("arr", 0, 6), ("arr", 0, 8), ("arr", 0, 7), ("prod", 1, 0), ("arr", 0, 9),
+    ("arr", 0, 10), ("prod", 0, 1), ("arr", 1, 5), ("arr", 1, 10), ("arr", 1, 7), ("prod", 0, 3),
+    ("prod", 0, 2), ("arr", 1, 6), ("arr", 0, 12), ("arr", 0, 11), ("prod", 0, 4), ("arr", 1, 8),
+    ("arr", 1, 9), ("arr", 0, 13), ("arr", 0, 14), ("arr", 0, 15), ("prod", 0, 0), ("prod", 0, 5),
+    ("prod", 0, 6), ("prod", 0, 7), ("hidden", 0), ("arr", 1, 13), ("arr", 1, 15), ("arr", 1, 11),
+    ("down",), ("pre2", 0), ("arr", 1, 12), ("prod", 1, 3), ("prod", 1, 2), ("arr", 1, 14),
+    ("p2", 0), ("ahead", 0, 0), ("ahead", 0, 1), ("pd", 0, 1), ("prod", 1, 6), ("direct", 0, 0, 1),
+    ("prod", 1, 7), ("pd", 0, 0), ("direct", 0, 1, 0), ("direct", 0, 1, 1), ("prod", 1, 4), ("direct", 0, 0, 0),
+    ("prod", 1, 5), ("hidden", 1), ("pre2", 1), ("joined", 0, 0, 0), ("joined", 0, 0, 1), ("joined", 0, 1, 0),
+    ("joined", 0, 1, 1), ("p2", 1), ("ahead", 1, 0), ("ahead", 1, 1), ("p0", 0), ("pd", 1, 0),
+    ("pd", 1, 1), ("direct", 1, 0, 0), ("direct", 1, 0, 1), ("direct", 1, 1, 1), ("direct", 1, 1, 0), ("sum", 0, 0),
+    ("sum", 0, 2), ("sum", 0, 1), ("joined", 1, 0, 0), ("p0", 1), ("joined", 1, 0, 1), ("own", 0),
+    ("joined", 1, 1, 0), ("joined", 1, 1, 1), ("finish", 0), ("sum", 1, 0), ("sum", 1, 2), ("own", 1),
+    ("sum", 1, 1), ("finish", 1),
 )
 
 
@@ -172,9 +172,11 @@
         if j == 0:
             pass_on(h, i, j, None, to_b(1), 0, 1)
             pass_on(h, i, j, None, to_b(3), 0, 3)
-        if j == 3:
+        if (i, j) == (2, 0):
+            pass_on(h, i, j, None, to_b(2), 0, 2)
+        if j == 3 and i != 2:
             pass_on(h, i, j, 0, to_b(1), 0, 1)
-        if j == 1:
+        if j == 1 and i != 2:
             pass_on(h, i, j, 1, to_b(3), 0, 3)
         group = next(g for g, pair in enumerate(PRODUCTS) if MIRROR[n] in pair)
         remote(gathered.at[h, c, k], gathered.at[h, c, k], d_s, d_r.at[h, group], mate)
@@ -198,13 +200,13 @@
                 xn[p, :, lanes] = normed.astype(jnp.bfloat16)
             offsets.append(at)
         for n in (0, 1):
-            terms = sum(dot(xn[p], wide_w[n, :, at], ((1,), (1,))) for p, at in enumerate(offsets))
+            terms = sum(dot(wide_w[n, :, at], xn[p], ((1,), (1,))) for p, at in enumerate(offsets))
             sums[h, n] = sums[h, n] + terms if h in opened else terms
         opened.add(h)
 
     def hidden(h):
         g = sums[h, 0]
-        hid[h, c] = (g / (1.0 + jnp.exp(-g)) * sums[h, 1]).astype(jnp.bfloat16)
+        hid[h, c] = (g / (1.0 + jnp.exp(-g)) * sums[h, 1]).T.astype(jnp.bfloat16)
         remote(hid.at[h, c], hid.at[h, c], h_s, h_r.at[h], mate)
 
     AHEAD, STEP, SIDES = 2, (1, 3), (1, 3)
@@ -377,7 +379,7 @@
             pltpu.VMEM((FEAT, FEAT), f32),
             pltpu.VMEM((10, 1, FEAT), f32),
             pltpu.VMEM((2, HALF, 2 * FEAT), bf16),
-            pltpu.VMEM((2, 2, HALF, HID), f32),
+            pltpu.VMEM((2, 2, HID, HALF), f32),
             pltpu.VMEM((2, 2, HALF, HID), bf16),
             pltpu.VMEM((2, SIDE, HALF, SIDE * FEAT), f32),
             pltpu.VMEM((2, 2, QUARTER, FEAT), f32),

time: 58.5 us -> 56.6 us (0.968)
  the two profiles are of different devices: /device:TPU:1 before, /device:TPU:2 now
where the time goes in v3:
time: 56.6 us; the launch traced here: 56 us
  Pallas kernels  51.9 us (92%)
  local copies, waits for them, and re-layouts  4.08 us (7%)
    pallas_call x1, Pallas kernels, local(): pl.pallas_call(kernel, out_shape=jax.ShapeDtypeStruct((FEAT, FEAT), bf16)...  51.9 us
    unnamed x11, local copies, waits for them, and re-layouts  4.08 us

profile of v3, /device:TPU:2, one launch (start us, length us, event | category | flops | bytes accessed | tf_op | source)
XLA Modules:
  0.0 56.0 jit_solution(3586767451237125381)
XLA Ops:
  0.0 0.0 copy-start
  0.0 0.8 %copy-done = bf16[128,128]{1,0:T(8,128)(2,1)S(1)} copy-done((bf16[128,128]{1,0:T(8,128)(2,1)S(1)}, bf16[128,128]{1,0:T(8,128)(2,1)}, u32[]{:S(2)}) %copy-start) | copy-done | bytes 32792
  0.8 0.0 copy-start.1
  0.8 0.7 %copy-done.1 = bf16[4096]{0:T(1024)(128)(2,1)S(1)} copy-done((bf16[4096]{0:T(1024)(128)(2,1)S(1)}, bf16[4096]{0:T(1024)(128)(2,1)}, u32[]{:S(2)}) %copy-start.1) | copy-done | bytes 8216
  1.5 0.0 copy-start.2
  1.5 0.7 %copy-done.2 = f32[128,2]{0,1:T(2,128)S(1)} copy-done((f32[128,2]{0,1:T(2,128)S(1)}, f32[128,2]{0,1:T(2,128)}, u32[]{:S(2)}) %copy-start.2) | copy-done | bytes 1048
  2.1 0.0 copy-start.3
  2.1 0.7 %copy-done.3 = s32[128,2]{0,1:T(2,128)S(1)} copy-done((s32[128,2]{0,1:T(2,128)S(1)}, s32[128,2]{0,1:T(2,128)}, u32[]{:S(2)}) %copy-start.3) | copy-done | bytes 1048
  2.8 0.0 copy-start.4
  2.8 0.7 %copy-done.4 = s32[128]{0:T(128)S(1)} copy-done((s32[128]{0:T(128)S(1)}, s32[128]{0:T(128)}, u32[]{:S(2)}) %copy-start.4) | copy-done | bytes 536
  3.5 51.9 %shard_map.82 = bf16[128,128]{1,0:T(8,128)(2,1)S(1)} custom-call(bf16[128,128]{1,0:T(8,128)(2,1)S(1)} %copy-done, bf16[4096]{0:T(1024)(128)(2,1)S(1)} %copy-done.1, f32[2,128]{1,0:T(2,128)S(1)} %bitcast.6, s32[2,128]{1,0:T(2,128)S(1)} %bitcast.7, s32[1,128]{1,0:T(1,128)S(1)} %bitcast.8, bf16[448,4096]{1,0:T(8,128)(2,1)} %bitcast.9, ...), custom_call_target="tpu_custom_call" | custom-call | tf_op jit(solution)/shard_map/pallas_call | solution.py:366
  55.4 0.6 %copy.10 = bf16[128,128]{1,0:T(8,128)(2,1)} copy(bf16[128,128]{1,0:T(8,128)(2,1)S(1)} %shard_map.82) | data formatting | bytes 65536
Async XLA Ops:
  0.0 0.8 %copy-start = (bf16[128,128]{1,0:T(8,128)(2,1)S(1)}, bf16[128,128]{1,0:T(8,128)(2,1)}, u32[]{:S(2)}) copy-start(bf16[128,128]{1,0:T(8,128)(2,1)} %tok_ref.1) | copy-start | bytes 98308
  0.8 0.7 %copy-start.1 = (bf16[4096]{0:T(1024)(128)(2,1)S(1)}, bf16[4096]{0:T(1024)(128)(2,1)}, u32[]{:S(2)}) copy-start(bf16[4096]{0:T(1024)(128)(2,1)} %gain_ref.1) | copy-start | bytes 24580
  1.5 0.7 %copy-start.2 = (f32[128,2]{0,1:T(2,128)S(1)}, f32[128,2]{0,1:T(2,128)}, u32[]{:S(2)}) copy-start(f32[128,2]{0,1:T(2,128)} %param.10) | copy-start | bytes 3076
  2.1 0.7 %copy-start.3 = (s32[128,2]{0,1:T(2,128)S(1)}, s32[128,2]{0,1:T(2,128)}, u32[]{:S(2)}) copy-start(s32[128,2]{0,1:T(2,128)} %param.11) | copy-start | bytes 3076
  2.8 0.7 %copy-start.4 = (s32[128]{0:T(128)S(1)}, s32[128]{0:T(128)}, u32[]{:S(2)}) copy-start(s32[128]{0:T(128)} %param.12) | copy-start | bytes 1540

commit v4 on v3

--- a/solution.py
+++ b/solution.py
@@ -25,22 +25,22 @@
 BLOCKS = ((2, 3), (1, 0))
 
 SCHEDULE = (
-    ("arr", 0, 1), ("arr", 0, 2), ("arr", 0, 3), ("arr", 1, 4), ("arr", 1, 3), ("arr", 0, 4),
-    ("arr", 1, 1), ("scale", 0), ("arr", 0, 5), ("arr", 1, 2), ("scale", 1), ("weights",),
-    ("prod", 1, 1), ("arr", 0, 6), ("arr", 0, 8), ("arr", 0, 7), ("prod", 1, 0), ("arr", 0, 9),
-    ("arr", 0, 10), ("prod", 0, 1), ("arr", 1, 5), ("arr", 1, 10), ("arr", 1, 7), ("prod", 0, 3),
-    ("prod", 0, 2), ("arr", 1, 6), ("arr", 0, 12), ("arr", 0, 11), ("prod", 0, 4), ("arr", 1, 8),
-    ("arr", 1, 9), ("arr", 0, 13), ("arr", 0, 14), ("arr", 0, 15), ("prod", 0, 0), ("prod", 0, 5),
-    ("prod", 0, 6), ("prod", 0, 7), ("hidden", 0), ("arr", 1, 13), ("arr", 1, 15), ("arr", 1, 11),
-    ("down",), ("pre2", 0), ("arr", 1, 12), ("prod", 1, 3), ("prod", 1, 2), ("arr", 1, 14),
-    ("p2", 0), ("ahead", 0, 0), ("ahead", 0, 1), ("pd", 0, 1), ("prod", 1, 6), ("direct", 0, 0, 1),
-    ("prod", 1, 7), ("pd", 0, 0), ("direct", 0, 1, 0), ("direct", 0, 1, 1), ("prod", 1, 4), ("direct", 0, 0, 0),
-    ("prod", 1, 5), ("hidden", 1), ("pre2", 1), ("joined", 0, 0, 0), ("joined", 0, 0, 1), ("joined", 0, 1, 0),
-    ("joined", 0, 1, 1), ("p2", 1), ("ahead", 1, 0), ("ahead", 1, 1), ("p0", 0), ("pd", 1, 0),
-    ("pd", 1, 1), ("direct", 1, 0, 0), ("direct", 1, 0, 1), ("direct", 1, 1, 1), ("direct", 1, 1, 0), ("sum", 0, 0),
-    ("sum", 0, 2), ("sum", 0, 1), ("joined", 1, 0, 0), ("p0", 1), ("joined", 1, 0, 1), ("own", 0),
-    ("joined", 1, 1, 0), ("joined", 1, 1, 1), ("finish", 0), ("sum", 1, 0), ("sum", 1, 2), ("own", 1),
-    ("sum", 1, 1), ("finish", 1),
+    ("arr", 0, 1), ("arr", 0, 2), ("arr", 0, 4), ("arr", 0, 3), ("arr", 0, 5), ("scale", 0),
+    ("arr", 1, 1), ("arr", 0, 7), ("arr", 0, 6), ("arr", 0, 9), ("arr", 0, 8), ("weights",),
+    ("prod", 0, 1), ("arr", 0, 10), ("arr", 1, 4), ("arr", 1, 2), ("prod", 0, 3), ("arr", 1, 5),
+    ("prod", 0, 2), ("arr", 1, 3), ("prod", 0, 0), ("arr", 0, 12), ("scale", 1), ("arr", 0, 15),
+    ("arr", 1, 7), ("arr", 0, 11), ("arr", 0, 13), ("prod", 0, 4), ("arr", 0, 14), ("arr", 1, 6),
+    ("prod", 1, 0), ("prod", 0, 7), ("prod", 0, 5), ("prod", 0, 6), ("hidden", 0), ("arr", 1, 9),
+    ("down",), ("pre2", 0), ("arr", 1, 11), ("arr", 1, 12), ("arr", 1, 8), ("prod", 1, 1),
+    ("arr", 1, 10), ("prod", 1, 3), ("p2", 0), ("ahead", 0, 0), ("ahead", 0, 1), ("pd", 0, 0),
+    ("arr", 1, 15), ("prod", 1, 4), ("prod", 1, 2), ("arr", 1, 13), ("pd", 0, 1), ("arr", 1, 14),
+    ("direct", 0, 1, 1), ("direct", 0, 1, 0), ("prod", 1, 7), ("direct", 0, 0, 1), ("prod", 1, 5), ("direct", 0, 0, 0),
+    ("prod", 1, 6), ("hidden", 1), ("joined", 0, 0, 1), ("joined", 0, 0, 0), ("joined", 0, 1, 1), ("joined", 0, 1, 0),
+    ("pre2", 1), ("p2", 1), ("ahead", 1, 0), ("ahead", 1, 1), ("pd", 1, 1), ("pd", 1, 0),
+    ("direct", 1, 1, 0), ("direct", 1, 0, 1), ("direct", 1, 0, 0), ("p0", 0), ("direct", 1, 1, 1), ("p0", 1),
+    ("sum", 0, 0), ("sum", 0, 1), ("sum", 0, 2), ("joined", 1, 0, 1), ("own", 0), ("joined", 1, 0, 0),
+    ("joined", 1, 1, 1), ("joined", 1, 1, 0), ("finish", 0), ("sum", 1, 0), ("sum", 1, 2), ("sum", 1, 1),
+    ("own", 1), ("finish", 1),
 )
 
 
@@ -73,10 +73,11 @@
 
 
 def kernel(
-    tok_ref, gain_ref, logit_ref, ids_ref, act_ref, wg_hbm, wu_hbm, wd_hbm, out_ref,
+    tok_hbm, gain_hbm, logit_hbm, ids_hbm, act_hbm, wg_hbm, wu_hbm, wd_hbm, out_ref,
+    tok_ref, gain_ref, logit_ref, ids_ref, act_ref,
     wide_w, dn, outbox, gathered, scale_rows, rsend, rrecv, turned, msb, xn, sums, hid, part, red,
     sfb, sdb, rfb, rdb, sda, rda, fin, ret,
-    w_sem, dn_sem, dns_sem, dnr_sem, z_s, z_r, rz_s, rz_r, ms_s, ms_r, g_s, g_r, d_s, d_r, h_s, h_r,
+    in_sem, w_sem, dn_sem, dns_sem, dnr_sem, z_s, z_r, rz_s, rz_r, ms_s, ms_r, g_s, g_r, d_s, d_r, h_s, h_r,
     bf_s, bf_r, bd_s, bd_r, ad_s, ad_r, t_s, t_r,
 ):
     z, x, y, c = (lax.axis_index(n) for n in ("expert", "x", "y", "c"))
@@ -102,19 +103,24 @@
     def arrived(ref, sem):
         pltpu.make_async_copy(ref, ref, sem).wait()
 
-    for n, w in enumerate((wg_hbm, wu_hbm)):
-        pltpu.make_async_copy(w, wide_w.at[n], w_sem).start()
-
     def down_columns(aa, bb, core):
         xx = jnp.where(core == 0, aa, bb)
         yy = jnp.where(core == 0, bb, aa)
         return pl.ds(pl.multiple_of(((xx * SIDE + yy) * 2 + core) * FEAT, FEAT), FEAT)
 
+    small = ((tok_hbm, tok_ref), (act_hbm, act_ref), (ids_hbm, ids_ref), (logit_hbm, logit_ref), (gain_hbm, gain_ref))
+    small = [pltpu.make_async_copy(source, target, in_sem.at[n]) for n, (source, target) in enumerate(small)]
+    for copy in small:
+        copy.start()
     barrier = pltpu.get_barrier_semaphore()
     peers = [mate] + [{"x": wrap(x + s)} for s in (1, 2, 3)] + [{"y": wrap(y + s)} for s in (1, 2, 3)] + [to_z(s) for s in range(1, ZS)]
     for peer in peers:
         pl.semaphore_signal(barrier, inc=1, device_id=peer, device_id_type=MESH)
 
+    for copy in small[:3]:
+        copy.wait()
+    for n, w in enumerate((wg_hbm, wu_hbm)):
+        pltpu.make_async_copy(w, wide_w.at[n], w_sem).start()
     for aa in range(SIDE):
         for bb in range(SIDE):
             pltpu.make_async_copy(wd_hbm.at[:, down_columns(aa, bb, c)], dn.at[c, bb, :, pl.ds(aa * FEAT, FEAT)], dn_sem).start()
@@ -287,6 +293,8 @@
     for s in range(1, ZS):
         remote(rsend, rrecv.at[z], rz_s, rz_r.at[my_half], to_z(s))
     pltpu.make_async_copy(rsend, rrecv.at[z], rz_r.at[my_half]).start()
+    for copy in small[3:]:
+        copy.wait()
     l0, l1 = logit_ref[0:1, :], logit_ref[1:2, :]
     high = jnp.maximum(l0, l1)
     e0, e1 = jnp.exp(l0 - high), jnp.exp(l1 - high)
@@ -363,12 +371,21 @@
     bf16, f32, i16 = jnp.bfloat16, jnp.float32, jnp.int16
     dma = pltpu.SemaphoreType.DMA
     double = 2 * QUARTER + 16
+
+    def pin(v):
+        return pltpu.with_memory_space_constraint(v, pltpu.HBM)
+
     return pl.pallas_call(
         kernel,
         out_shape=jax.ShapeDtypeStruct((FEAT, FEAT), bf16),
-        in_specs=[vmem] * 5 + [hbm] * 3,
+        in_specs=[hbm] * 8,
         out_specs=vmem,
         scratch_shapes=[
+            pltpu.VMEM((FEAT, FEAT), bf16),
+            pltpu.VMEM((WIDTH,), bf16),
+            pltpu.VMEM((2, FEAT), f32),
+            pltpu.VMEM((2, FEAT), jnp.int32),
+            pltpu.VMEM((1, FEAT), jnp.int32),
             pltpu.VMEM((2, HID, WIDTH), bf16),
             pltpu.VMEM((2, SIDE, HID, SIDE * FEAT), bf16),
             pltpu.VMEM((ROWS, FEAT), bf16),
@@ -391,7 +408,7 @@
             pltpu.VMEM((2, 3, double, FEAT), i16),
             pltpu.VMEM((2, HALF, FEAT), bf16),
             pltpu.VMEM((ROWS, FEAT), bf16),
-            dma, dma, dma, dma,
+            dma((5,)), dma, dma, dma, dma,
             dma, dma((2,)), dma, dma((2,)), dma, dma((3,)),
             dma, dma((2, 16)), dma, dma((2, 8)), dma, dma((2,)),
             dma, dma((2, 2, 2)), dma, dma((2, 2)), dma, dma((2,)),
@@ -399,11 +416,11 @@
         ],
         compiler_params=pltpu.CompilerParams(collective_id=0, has_side_effects=True, vmem_limit_bytes=52 * 1024 * 1024),
     )(
-        tokens,
-        norm_gain,
-        route_logits.T,
-        expert_ids.T,
-        active.reshape(1, FEAT),
+        pin(tokens),
+        pin(norm_gain),
+        pin(route_logits.T),
+        pin(expert_ids.T),
+        pin(active.reshape(1, FEAT)),
         gate_weight.reshape(HID, WIDTH),
         up_weight.reshape(HID, WIDTH),
         down_weight.reshape(HID, WIDTH),

time: 56.6 us -> 52.7 us (0.931)
  local copies, waits for them, and re-layouts: 4.08 us -> 0.62 us
    unnamed x11 -> x1, local copies, waits for them, and re-layouts: 4.08 us -> 0.62 us
where the time goes in v4:
time: 52.7 us; the launch traced here: 52.6 us
  Pallas kernels  52 us (99%)
  local copies, waits for them, and re-layouts  0.62 us (1%)
    pallas_call x1, Pallas kernels, local(): pl.pallas_call(kernel, out_shape=jax.ShapeDtypeStruct((FEAT, FEAT), bf16)...  52 us

profile of v4, /device:TPU:2, one launch (start us, length us, event | category | flops | bytes accessed | tf_op | source)
XLA Modules:
  0.0 52.6 jit_solution(2164193613124659704)
XLA Ops:
  0.0 52.0 %shard_map.82 = bf16[128,128]{1,0:T(8,128)(2,1)S(1)} custom-call(bf16[128,128]{1,0:T(8,128)(2,1)} %tok_hbm.1, bf16[4096]{0:T(1024)(128)(2,1)} %gain_hbm.1, f32[2,128]{1,0:T(2,128)} %bitcast.9, s32[2,128]{1,0:T(2,128)} %bitcast.10, s32[1,128]{1,0:T(1,128)} %bitcast.11, bf16[448,4096]{1,0:T(8,128)(2,1)} %bitcast.6, bf16[448,4096]{1,0:T(8,128)(2,1)} %bitcast.7, ...), custom_call_target="tpu_custom_call" | custom-call | tf_op jit(solution)/shard_map/pallas_call | solution.py:378
  52.0 0.6 %copy.10 = bf16[128,128]{1,0:T(8,128)(2,1)} copy(bf16[128,128]{1,0:T(8,128)(2,1)S(1)} %shard_map.82) | data formatting | bytes 65536

commit v5 on v4

--- a/solution.py
+++ b/solution.py
@@ -25,21 +25,21 @@
 BLOCKS = ((2, 3), (1, 0))
 
 SCHEDULE = (
-    ("arr", 0, 1), ("arr", 0, 2), ("arr", 0, 4), ("arr", 0, 3), ("arr", 0, 5), ("scale", 0),
-    ("arr", 1, 1), ("arr", 0, 7), ("arr", 0, 6), ("arr", 0, 9), ("arr", 0, 8), ("weights",),
-    ("prod", 0, 1), ("arr", 0, 10), ("arr", 1, 4), ("arr", 1, 2), ("prod", 0, 3), ("arr", 1, 5),
-    ("prod", 0, 2), ("arr", 1, 3), ("prod", 0, 0), ("arr", 0, 12), ("scale", 1), ("arr", 0, 15),
-    ("arr", 1, 7), ("arr", 0, 11), ("arr", 0, 13), ("prod", 0, 4), ("arr", 0, 14), ("arr", 1, 6),
-    ("prod", 1, 0), ("prod", 0, 7), ("prod", 0, 5), ("prod", 0, 6), ("hidden", 0), ("arr", 1, 9),
-    ("down",), ("pre2", 0), ("arr", 1, 11), ("arr", 1, 12), ("arr", 1, 8), ("prod", 1, 1),
-    ("arr", 1, 10), ("prod", 1, 3), ("p2", 0), ("ahead", 0, 0), ("ahead", 0, 1), ("pd", 0, 0),
-    ("arr", 1, 15), ("prod", 1, 4), ("prod", 1, 2), ("arr", 1, 13), ("pd", 0, 1), ("arr", 1, 14),
-    ("direct", 0, 1, 1), ("direct", 0, 1, 0), ("prod", 1, 7), ("direct", 0, 0, 1), ("prod", 1, 5), ("direct", 0, 0, 0),
-    ("prod", 1, 6), ("hidden", 1), ("joined", 0, 0, 1), ("joined", 0, 0, 0), ("joined", 0, 1, 1), ("joined", 0, 1, 0),
-    ("pre2", 1), ("p2", 1), ("ahead", 1, 0), ("ahead", 1, 1), ("pd", 1, 1), ("pd", 1, 0),
-    ("direct", 1, 1, 0), ("direct", 1, 0, 1), ("direct", 1, 0, 0), ("p0", 0), ("direct", 1, 1, 1), ("p0", 1),
+    ("arr", 0, 1), ("arr", 0, 2), ("arr", 0, 4), ("arr", 0, 3), ("arr", 0, 5), ("arr", 1, 1),
+    ("arr", 0, 7), ("arr", 0, 6), ("arr", 0, 9), ("arr", 0, 8), ("arr", 1, 2), ("scale", 0),
+    ("arr", 0, 10), ("scale", 1), ("weights",), ("prod", 0, 0), ("arr", 1, 3), ("arr", 1, 5),
+    ("prod", 0, 3), ("prod", 0, 2), ("arr", 0, 11), ("arr", 1, 4), ("prod", 0, 4), ("arr", 0, 12),
+    ("prod", 0, 1), ("arr", 0, 15), ("arr", 1, 7), ("arr", 1, 6), ("arr", 0, 13), ("prod", 1, 1),
+    ("arr", 0, 14), ("prod", 0, 7), ("prod", 0, 5), ("prod", 0, 6), ("hidden", 0), ("arr", 1, 12),
+    ("down",), ("pre2", 0), ("arr", 1, 9), ("arr", 1, 11), ("arr", 1, 8), ("prod", 1, 0),
+    ("arr", 1, 10), ("prod", 1, 3), ("p2", 0), ("ahead", 0, 0), ("ahead", 0, 1), ("prod", 1, 4),
+    ("arr", 1, 15), ("pd", 0, 1), ("pd", 0, 0), ("direct", 0, 0, 1), ("arr", 1, 13), ("prod", 1, 2),
+    ("direct", 0, 1, 1), ("direct", 0, 0, 0), ("arr", 1, 14), ("prod", 1, 7), ("direct", 0, 1, 0), ("p0", 0),
+    ("prod", 1, 5), ("prod", 1, 6), ("hidden", 1), ("joined", 0, 0, 1), ("joined", 0, 0, 0), ("pre2", 1),
+    ("joined", 0, 1, 1), ("joined", 0, 1, 0), ("p2", 1), ("ahead", 1, 0), ("p0", 1), ("ahead", 1, 1),
+    ("pd", 1, 0), ("pd", 1, 1), ("direct", 1, 0, 1), ("direct", 1, 0, 0), ("direct", 1, 1, 0), ("direct", 1, 1, 1),
     ("sum", 0, 0), ("sum", 0, 1), ("sum", 0, 2), ("joined", 1, 0, 1), ("own", 0), ("joined", 1, 0, 0),
-    ("joined", 1, 1, 1), ("joined", 1, 1, 0), ("finish", 0), ("sum", 1, 0), ("sum", 1, 2), ("sum", 1, 1),
+    ("joined", 1, 1, 0), ("joined", 1, 1, 1), ("finish", 0), ("sum", 1, 0), ("sum", 1, 2), ("sum", 1, 1),
     ("own", 1), ("finish", 1),
 )
 
@@ -76,8 +76,8 @@
     tok_hbm, gain_hbm, logit_hbm, ids_hbm, act_hbm, wg_hbm, wu_hbm, wd_hbm, out_ref,
     tok_ref, gain_ref, logit_ref, ids_ref, act_ref,
     wide_w, dn, outbox, gathered, scale_rows, rsend, rrecv, turned, msb, xn, sums, hid, part, red,
-    sfb, sdb, rfb, rdb, sda, rda, fin, ret,
-    in_sem, w_sem, dn_sem, dns_sem, dnr_sem, z_s, z_r, rz_s, rz_r, ms_s, ms_r, g_s, g_r, d_s, d_r, h_s, h_r,
+    sfb, sdb, rfb, rdb, sda, rda, fin, ret, picks,
+    w_sem, dn_sem, dns_sem, dnr_sem, z_s, z_r, rz_s, rz_r, ms_s, ms_r, g_s, g_r, d_s, d_r, h_s, h_r,
     bf_s, bf_r, bd_s, bd_r, ad_s, ad_r, t_s, t_r,
 ):
     z, x, y, c = (lax.axis_index(n) for n in ("expert", "x", "y", "c"))
@@ -109,11 +109,12 @@
         return pl.ds(pl.multiple_of(((xx * SIDE + yy) * 2 + core) * FEAT, FEAT), FEAT)
 
     small = ((tok_hbm, tok_ref), (act_hbm, act_ref), (ids_hbm, ids_ref), (logit_hbm, logit_ref), (gain_hbm, gain_ref))
-    small = [pltpu.make_async_copy(source, target, in_sem.at[n]) for n, (source, target) in enumerate(small)]
+    small = [pltpu.make_async_copy(source, target, sem) for (source, target), sem in zip(small, (h_s, bf_s, bd_s, ad_s, t_s))]
     for copy in small:
         copy.start()
     barrier = pltpu.get_barrier_semaphore()
-    peers = [mate] + [{"x": wrap(x + s)} for s in (1, 2, 3)] + [{"y": wrap(y + s)} for s in (1, 2, 3)] + [to_z(s) for s in range(1, ZS)]
+    chips = [{"x": wrap(x + n // SIDE), "y": wrap(y + n % SIDE)} for n in range(1, SIDE * SIDE)]
+    peers = [mate] + chips + [to_z(s) for s in range(1, ZS)]
     for peer in peers:
         pl.semaphore_signal(barrier, inc=1, device_id=peer, device_id_type=MESH)
 
@@ -144,6 +145,8 @@
     pick = (pick0 + pick1).astype(jnp.bfloat16)
     outbox[...] = dot(pick, tok, ((1,), (0,))).astype(jnp.bfloat16)
 
+    picks[0] = pick0.T.astype(jnp.bfloat16)
+    picks[1] = pick1.T.astype(jnp.bfloat16)
     pl.semaphore_wait(barrier, len(peers))
     remote(msb.at[0], msb.at[1], ms_s, ms_r.at[0], mate)
     me = a * SIDE + b
@@ -278,16 +281,12 @@
 
     arrived(msb.at[1], ms_r.at[0])
     msb[2] = msb[0] + msb[1]
-    for s in (1, 2, 3):
-        remote(msb.at[2], msb.at[2 + s], ms_s, ms_r.at[1], {"x": wrap(x + s)})
-    arrived(msb.at[pl.ds(3, 3)], ms_r.at[1])
-    msb[6] = (msb[2] + msb[3]) + (msb[4] + msb[5])
-    for s in (1, 2, 3):
-        remote(msb.at[6], msb.at[6 + s], ms_s, ms_r.at[2], {"y": wrap(y + s)})
+    for n, chip in enumerate(chips):
+        remote(msb.at[2], msb.at[3 + n], ms_s, ms_r.at[1], chip)
     arrive(0, 0)
     arrive(1, 0)
-    arrived(msb.at[pl.ds(7, 3)], ms_r.at[2])
-    mean_square = ((msb[6] + msb[7]) + (msb[8] + msb[9])) / WIDTH
+    arrived(msb.at[pl.ds(3, 15)], ms_r.at[1])
+    mean_square = jnp.sum(msb[2:18], axis=0) / WIDTH
     inverse = lax.rsqrt(mean_square + EPS)
     rsend[...] = dot(jnp.broadcast_to(inverse, (8, FEAT)), pick.astype(jnp.float32), ((1,), (1,)), lax.Precision.HIGHEST)[0:1, :]
     for s in range(1, ZS):
@@ -323,8 +322,8 @@
         partial(h, AHEAD, False, False)
 
     def whole_partial(h, j):
-        partial(h, j, True, True)
-        partial(h, j, False, False)
+        bb = wrap(b + j)
+        part[h, j] = dot(hid[h, 0], dn[0, bb], ((1,), (0,))) + dot(hid[h, 1], dn[1, bb], ((1,), (0,)))
 
     events = {
         "arr": arrive,
@@ -348,13 +347,13 @@
         events[name](*which)
     arrived(ret, t_r)
     back = ret[...]
-    from0 = dot(pick0.astype(jnp.bfloat16), back, ((0,), (0,)))
-    from1 = dot(pick1.astype(jnp.bfloat16), back, ((0,), (0,)))
+    from0 = dot(picks[0], back, ((1,), (0,)))
+    from1 = dot(picks[1], back, ((1,), (0,)))
     out_ref[...] = (prob0 * from0 + prob1 * from1).astype(jnp.bfloat16)
 
     arrived(outbox.at[pl.ds(0, ROWS - SEATS)], z_s)
     arrived(rrecv.at[pl.ds(0, ZS - 1)], rz_s)
-    arrived(msb.at[pl.ds(0, 7)], ms_s)
+    arrived(msb.at[pl.ds(0, 16)], ms_s)
     arrived(gathered.at[:, 0, pl.ds(0, 15)], g_s)
     arrived(gathered.at[:, 0], d_s)
     arrived(hid.at[:, 0], h_s)
@@ -394,7 +393,7 @@
             pltpu.VMEM((1, ROWS), f32),
             pltpu.VMEM((ZS, 1, ROWS), f32),
             pltpu.VMEM((FEAT, FEAT), f32),
-            pltpu.VMEM((10, 1, FEAT), f32),
+            pltpu.VMEM((18, 1, FEAT), f32),
             pltpu.VMEM((2, HALF, 2 * FEAT), bf16),
             pltpu.VMEM((2, 2, HID, HALF), f32),
             pltpu.VMEM((2, 2, HALF, HID), bf16),
@@ -408,8 +407,9 @@
             pltpu.VMEM((2, 3, double, FEAT), i16),
             pltpu.VMEM((2, HALF, FEAT), bf16),
             pltpu.VMEM((ROWS, FEAT), bf16),
-            dma((5,)), dma, dma, dma, dma,
-            dma, dma((2,)), dma, dma((2,)), dma, dma((3,)),
+            pltpu.VMEM((2, FEAT, ROWS), bf16),
+            dma, dma, dma, dma,
+            dma, dma((2,)), dma, dma((2,)), dma, dma((2,)),
             dma, dma((2, 16)), dma, dma((2, 8)), dma, dma((2,)),
             dma, dma((2, 2, 2)), dma, dma((2, 2)), dma, dma((2,)),
             dma, dma,

time: 52.7 us -> 51.3 us (0.973)
  Pallas kernels: 52 us -> 50.3 us
    pallas_call x1, Pallas kernels: 52 us -> 50.3 us  [local(): pl.pallas_call(kernel, out_shape=jax.ShapeDtypeStruct((FEAT, FEAT), bf16)...]
where the time goes in v5:
time: 51.3 us; the launch traced here: 50.9 us
  Pallas kernels  50.3 us (98%)
  local copies, waits for them, and re-layouts  0.62 us (1%)
    pallas_call x1, Pallas kernels, local(): pl.pallas_call(kernel, out_shape=jax.ShapeDtypeStruct((FEAT, FEAT), bf16)...  50.3 us

profile of v5, /device:TPU:2, one launch (start us, length us, event | category | flops | bytes accessed | tf_op | source)
XLA Modules:
  0.0 50.9 jit_solution(8376552238746702798)
XLA Ops:
  0.0 50.3 %shard_map.82 = bf16[128,128]{1,0:T(8,128)(2,1)S(1)} custom-call(bf16[128,128]{1,0:T(8,128)(2,1)} %tok_hbm.1, bf16[4096]{0:T(1024)(128)(2,1)} %gain_hbm.1, f32[2,128]{1,0:T(2,128)} %bitcast.9, s32[2,128]{1,0:T(2,128)} %bitcast.10, s32[1,128]{1,0:T(1,128)} %bitcast.11, bf16[448,4096]{1,0:T(8,128)(2,1)} %bitcast.6, bf16[448,4096]{1,0:T(8,128)(2,1)} %bitcast.7, ...), custom_call_target="tpu_custom_call" | custom-call | tf_op jit(solution)/shard_map/pallas_call | solution.py:377
  50.3 0.6 %copy.10 = bf16[128,128]{1,0:T(8,128)(2,1)} copy(bf16[128,128]{1,0:T(8,128)(2,1)S(1)} %shard_map.82) | data formatting | bytes 65536

commit v6 on v5

--- a/solution.py
+++ b/solution.py
@@ -33,11 +33,11 @@
     ("arr", 0, 14), ("prod", 0, 7), ("prod", 0, 5), ("prod", 0, 6), ("hidden", 0), ("arr", 1, 12),
     ("down",), ("pre2", 0), ("arr", 1, 9), ("arr", 1, 11), ("arr", 1, 8), ("prod", 1, 0),
     ("arr", 1, 10), ("prod", 1, 3), ("p2", 0), ("ahead", 0, 0), ("ahead", 0, 1), ("prod", 1, 4),
-    ("arr", 1, 15), ("pd", 0, 1), ("pd", 0, 0), ("direct", 0, 0, 1), ("arr", 1, 13), ("prod", 1, 2),
-    ("direct", 0, 1, 1), ("direct", 0, 0, 0), ("arr", 1, 14), ("prod", 1, 7), ("direct", 0, 1, 0), ("p0", 0),
+    ("arr", 1, 15), ("pd", 0, 1), ("pd", 0, 0), ("direct", 0, 0, 1), ("direct", 0, 1, 0), ("direct", 0, 0, 0),
+    ("direct", 0, 1, 1), ("arr", 1, 13), ("prod", 1, 2), ("arr", 1, 14), ("prod", 1, 7), ("p0", 0),
     ("prod", 1, 5), ("prod", 1, 6), ("hidden", 1), ("joined", 0, 0, 1), ("joined", 0, 0, 0), ("pre2", 1),
-    ("joined", 0, 1, 1), ("joined", 0, 1, 0), ("p2", 1), ("ahead", 1, 0), ("p0", 1), ("ahead", 1, 1),
-    ("pd", 1, 0), ("pd", 1, 1), ("direct", 1, 0, 1), ("direct", 1, 0, 0), ("direct", 1, 1, 0), ("direct", 1, 1, 1),
+    ("joined", 0, 1, 1), ("joined", 0, 1, 0), ("p2", 1), ("ahead", 1, 0), ("ahead", 1, 1), ("pd", 1, 0),
+    ("pd", 1, 1), ("direct", 1, 0, 1), ("direct", 1, 0, 0), ("direct", 1, 1, 0), ("direct", 1, 1, 1), ("p0", 1),
     ("sum", 0, 0), ("sum", 0, 1), ("sum", 0, 2), ("joined", 1, 0, 1), ("own", 0), ("joined", 1, 0, 0),
     ("joined", 1, 1, 0), ("joined", 1, 1, 1), ("finish", 0), ("sum", 1, 0), ("sum", 1, 2), ("sum", 1, 1),
     ("own", 1), ("finish", 1),

time: 51.3 us -> 51.3 us (level)
  no operation moved by 1% of the time
where the time goes in v6:
time: 51.3 us; the launch traced here: 50.8 us
  Pallas kernels  50.2 us (98%)
  local copies, waits for them, and re-layouts  0.62 us (1%)
    pallas_call x1, Pallas kernels, local(): pl.pallas_call(kernel, out_shape=jax.ShapeDtypeStruct((FEAT, FEAT), bf16)...  50.2 us

profile of v6, /device:TPU:2, one launch (start us, length us, event | category | flops | bytes accessed | tf_op | source)
XLA Modules:
  0.0 50.8 jit_solution(3802074435155192522)
XLA Ops:
  0.0 50.2 %shard_map.82 = bf16[128,128]{1,0:T(8,128)(2,1)S(1)} custom-call(bf16[128,128]{1,0:T(8,128)(2,1)} %tok_hbm.1, bf16[4096]{0:T(1024)(128)(2,1)} %gain_hbm.1, f32[2,128]{1,0:T(2,128)} %bitcast.9, s32[2,128]{1,0:T(2,128)} %bitcast.10, s32[1,128]{1,0:T(1,128)} %bitcast.11, bf16[448,4096]{1,0:T(8,128)(2,1)} %bitcast.6, bf16[448,4096]{1,0:T(8,128)(2,1)} %bitcast.7, ...), custom_call_target="tpu_custom_call" | custom-call | tf_op jit(solution)/shard_map/pallas_call | solution.py:377
  50.2 0.6 %copy.10 = bf16[128,128]{1,0:T(8,128)(2,1)} copy(bf16[128,128]{1,0:T(8,128)(2,1)S(1)} %shard_map.82) | data formatting | bytes 65536
